TPU v7x, 8 devices: a whole 2x2x1 slice. The times are simulated.
8 devices in a mesh: frag: 1 (over z), dev2: 2 (over y), dev: 4 (over x, core).
Axes of the slice: x: 2, y: 2, z: 1, core: 2. Of those that a mesh axis runs over, the one named last changes fastest.
Arguments:
- ao_ints: bfloat16 [128, 128, 128, 128], P(('frag', 'dev'), 'dev2')
- c_occ: bfloat16 [128, 4], P('frag')
- c_virt: bfloat16 [128, 112], P('frag')
Outputs:
- output: float32 [4, 112, 448], P('frag', None, ('dev2', 'dev'))
All inputs are finite; a program needn't handle non-finite values.
Results may differ from a plain program's by a relative error of at most 0.001.
Values are sent between devices in bfloat16 or wider.
A program may use at most 1 GiB of HBM per device.

v0:
```python
import jax
import jax.numpy as jnp
from jax import lax
from jax.sharding import PartitionSpec as P


def solution(mesh):
    def local_block(ao_blk, c_occ, c_virt):
        occ_num = c_occ.shape[1]
        virt_num = c_virt.shape[1]
        t_one = jnp.einsum("pqrs,rj->pqsj", ao_blk, c_occ, preferred_element_type=jnp.float32).astype(jnp.bfloat16)
        half_blk = jnp.einsum("pqsj,sb->pqjb", t_one, c_virt, preferred_element_type=jnp.float32).astype(jnp.bfloat16)
        half_blk = half_blk.reshape(ao_blk.shape[0], ao_blk.shape[1], occ_num * virt_num)
        q_whole = lax.all_to_all(half_blk, "dev2", 2, 1, tiled=True)
        pq_whole = lax.all_to_all(q_whole, "dev", 2, 0, tiled=True)
        e_part = jnp.einsum("pi,pqk->iqk", c_occ, pq_whole, preferred_element_type=jnp.float32)
        return jnp.einsum("iqk,qa->iak", e_part, c_virt.astype(jnp.float32), precision=lax.Precision.HIGHEST, preferred_element_type=jnp.float32)

    return jax.shard_map(
        local_block, mesh=mesh,
        in_specs=(P(("frag", "dev"), "dev2", None, None), P("frag", None), P("frag", None)),
        out_specs=P("frag", None, ("dev2", "dev")),
        check_vma=False)
```

profile of v0, /device:TPU:0, one launch (start us, length us, event | category | flops | bytes accessed | tf_op | source)
XLA Modules:
  0.0 103.9 jit_solution(16545877084668063757)
XLA Ops:
  0.0 0.0 copy-start
  0.0 23.5 %convolution_convert_fusion = bf16[32,64,128,4]{2,3,1,0:T(4,128)(2,1)S(1)} fusion(bf16[32,64,128,128]{3,2,1,0:T(8,128)(2,1)} %param.3, bf16[128,4]{0,1:T(4,128)(2,1)} %param.4), kind=kOutput, calls=%fused_computation.2 | convolution fusion | flops 269484032 | bytes 69207040 | tf_op jit(solution)/shard_map/pqrs,rj->pqsj/dot_general | solution.py:11
  23.5 0.0 copy-done
  23.5 2.0 %fusion.2 = bf16[32,64,4,112]{3,1,2,0:T(8,128)(2,1)} fusion(bf16[32,64,128,4]{2,3,1,0:T(4,128)(2,1)S(1)} %convolution_convert_fusion, bf16[128,112]{0,1:T(8,128)(2,1)S(1)} %copy-done), kind=kOutput, calls=%fused_computation.3 | convolution fusion | flops 235798528 | bytes 3960832 | tf_op jit(solution)/shard_map/pqsj,sb->pqjb/dot_general | solution.py:12
  25.5 7.0 %copy.19 = bf16[32,64,4,112]{1,0,3,2:T(8,128)(2,1)} copy(bf16[32,64,4,112]{3,1,2,0:T(8,128)(2,1)} %fusion.2) | data formatting | bytes 3670016 | tf_op jit(solution)/shard_map/reshape | solution.py:13
  32.5 4.4 %reshape.8 = bf16[2,2,229376]{2,1,0:T(2,128)(2,1)S(1)} reshape(bf16[448,32,64]{2,1,0:T(8,128)(2,1)} %bitcast.32) | data formatting | bytes 3670016
  36.8 27.2 %all_to_all.36 = bf16[2,2,229376]{2,1,0:T(2,128)(2,1)} all-to-all(bf16[2,2,229376]{2,1,0:T(2,128)(2,1)S(1)} %reshape.8), channel_id=1, replica_groups=mesh['frag'=1,'dev2'=2,'dev'=4] {'dev2'}, dimensions={0} | all-to-all | bytes 3670016 | tf_op jit(solution)/shard_map/all_to_all | solution.py:14
  64.0 5.1 %reshape.9 = bf16[448,32,64]{2,1,0:T(8,128)(2,1)} reshape(bf16[2,2,229376]{2,1,0:T(2,128)(2,1)} %all_to_all.36) | data formatting | bytes 3670016
  69.2 4.2 %copy.11 = bf16[32,64,2,224]{3,1,2,0:T(8,128)(2,1)S(1)} copy(bf16[32,64,2,224]{1,0,3,2:T(8,128)(2,1)} %bitcast.33) | data formatting | bytes 3670016 | tf_op jit(solution)/shard_map/all_to_all | solution.py:14
  73.3 2.5 %copy.12 = bf16[32,128,224]{1,0,2:T(8,128)(2,1)} copy(bf16[32,128,224]{2,1,0:T(8,128)(2,1)S(1)} %bitcast.34) | data formatting | bytes 3670016 | tf_op jit(solution)/shard_map/all_to_all | solution.py:14
  75.8 26.2 %all_to_all.37 = bf16[32,128,224]{1,0,2:T(8,128)(2,1)S(1)} all-to-all(bf16[32,128,224]{1,0,2:T(8,128)(2,1)} %copy.12), channel_id=1, replica_groups=mesh['frag'=1,'dev2'=2,'dev'=4] {'dev'}, dimensions={2} | all-to-all | bytes 3670016 | tf_op jit(solution)/shard_map/all_to_all | solution.py:15
  102.0 0.0 copy-start.1
  102.0 0.7 copy.14
  102.7 0.0 copy-done.1
  102.7 0.4 fusion.7
  103.1 0.9 convolution_bitcast_fusion
Async XLA Ops:
  0.0 23.5 %copy-start = (bf16[128,112]{0,1:T(8,128)(2,1)S(1)}, bf16[128,112]{0,1:T(8,128)(2,1)}, u32[]{:S(2)}) copy-start(bf16[128,112]{0,1:T(8,128)(2,1)} %param.5) | copy-start | bytes 86020
  102.0 0.7 copy-start.1
where the time goes:
time: 104 us
  blocking collectives  53.4 us (51%)
  matrix products  26.7 us (26%)
  local copies, waits for them, and re-layouts  23.8 us (23%)
    all_to_all x1, blocking collectives, local_block(): q_whole = lax.all_to_all(half_blk, 'dev2', 2, 1, tiled=True)  27.2 us
    all_to_all x1, blocking collectives, local_block(): pq_whole = lax.all_to_all(q_whole, 'dev', 2, 0, tiled=True)  26.2 us
    dot_general x1, matrix products, local_block(): jnp.einsum('pqrs,rj->pqsj', ao_blk, c_occ, preferred_element_type=jnp.flo...  23.5 us
    unnamed x6, local copies, waits for them, and re-layouts  9.49 us
    reshape x1, local copies, waits for them, and re-layouts, local_block(): half_blk.reshape(ao_blk.shape[0], ao_blk.shape[1], occ_num * virt_num)  6.95 us
    all_to_all x2, local copies, waits for them, and re-layouts, local_block(): q_whole = lax.all_to_all(half_blk, 'dev2', 2, 1, tiled=True)  6.63 us

commit v1 on v0

v1 whole, which is shorter than its diff:
```python
import functools

import jax
import jax.numpy as jnp
from jax import lax
from jax.experimental import pallas as pl
from jax.experimental.pallas import tpu as pltpu
from jax.sharding import PartitionSpec as P

MESH = pl.DeviceIdType.MESH
F32 = jnp.float32
BF16 = jnp.bfloat16

ROWS_P = 32
ROWS_Q = 64
NBF = 128
OCC = 4
VIRT = 112
HALF = VIRT // 2
TILE_Q = 4
STEPS = ROWS_Q // TILE_Q
SLOTS = 8
DEVS = 8
COLS = 4


def iota(shape, dim):
    return lax.broadcasted_iota(jnp.int32, shape, dim)


def one_hot(cond):
    return jnp.where(cond, 1.0, 0.0).astype(BF16)


def dot(a, b):
    return jnp.dot(a, b, preferred_element_type=F32)


def dot_nt(a, b):
    return lax.dot_general(a, b, (((1,), (1,)), ((), ())), preferred_element_type=F32)


def dot_tn(a, b):
    return lax.dot_general(a, b, (((0,), (0,)), ((), ())), preferred_element_type=F32)


def kernel(a_hbm, co_hbm, cv_hbm, out_ref, abuf, co_ref, cv_ref, lhs1, cv2, w2, cvx, t1, sendbuf, recv,
           a_sem, c_sem, send_sem, recv_sem):
    row, col = lax.axis_index("dev2"), lax.axis_index("dev")
    me = row * COLS + col

    def fetch(step, slot):
        return pltpu.make_async_copy(a_hbm.at[:, pl.ds(step * TILE_Q, TILE_Q)], abuf.at[slot], a_sem.at[slot])

    co_copy = pltpu.make_async_copy(co_hbm, co_ref, c_sem.at[0])
    cv_copy = pltpu.make_async_copy(cv_hbm, cv_ref, c_sem.at[1])
    co_copy.start()
    cv_copy.start()
    for s in range(SLOTS):
        fetch(s, s).start()

    def peer(k):
        to = lax.rem(me + k, DEVS)
        return to, {"dev2": to // COLS, "dev": lax.rem(to, COLS)}

    barrier = pltpu.get_barrier_semaphore()
    for k in range(1, DEVS):
        pl.semaphore_signal(barrier, inc=1, device_id=peer(k)[1], device_id_type=MESH)

    co_copy.wait()
    cv_copy.wait()
    co, cv = co_ref[...], cv_ref[...]

    r16, c4 = iota((16, OCC), 0), iota((16, OCC), 1)
    co_t = dot_nt(one_hot(r16 % OCC == c4), co)
    r16 = iota((16, NBF), 0)
    lhs1[...] = jnp.concatenate(
        [jnp.where(r16 // OCC == k, co_t, 0.0) for k in range(2)], axis=1).astype(BF16)

    co_i = dot_nt(one_hot(iota((32, OCC), 0) % OCC == iota((32, OCC), 1)), co).astype(BF16)
    r, c = iota((NBF, 256), 0), iota((NBF, 256), 1)
    spread = dot(co_i, one_hot(r == col * ROWS_P + (c % NBF) // OCC))
    r, c = iota((32, 256), 0), iota((32, 256), 1)
    w2[...] = jnp.where(((r // OCC) % 2 == c // NBF) & (r // 8 == c % OCC), spread, 0.0).astype(BF16)

    b, c = iota((VIRT, 256), 0), iota((VIRT, 256), 1)
    halves = dot(cv, one_hot((b == (c // NBF) * HALF + c % 64) & (c % 64 < HALF)))
    c = iota((NBF, 256), 1)
    for par in range(2):
        cv2[par * NBF:(par + 1) * NBF, :] = jnp.where((c // 64) % 2 == par, halves, 0.0).astype(BF16)

    q, c = iota((NBF, 512), 0), iota((NBF, 512), 1)
    rows = dot_tn(cv, one_hot(q == ((c % 256) // OCC) * 2 + c // 256))
    c = iota((VIRT, 512), 1)
    for i in range(OCC):
        cvx[i * VIRT:(i + 1) * VIRT, :] = jnp.where(c % OCC == i, rows, 0.0).astype(BF16)

    pl.semaphore_wait(barrier, DEVS - 1)

    def step_body(step, carry):
        slot = lax.rem(step, SLOTS)
        fetch(step, slot).wait()
        left = lhs1[...]
        for qp in range(2):
            for pp in range(0, 16, 2):
                parts = []
                for p0 in (2 * pp, 2 * pp + 2):
                    rhs = jnp.concatenate(
                        [abuf[slot, p0:p0 + 2, 2 * qp + par].reshape(256, NBF) for par in range(2)], axis=1)
                    parts.append(dot(left, rhs)[:8])
                at = qp * 128 + pp * 8
                t1[at:at + 16, :] = jnp.concatenate(parts, axis=0).astype(BF16)
        half = dot(t1[...], cv2[...]).astype(BF16)
        e_part = dot(w2[...], half)
        for j in range(OCC):
            for h in range(2):
                sendbuf[step, 2 * j + h] = e_part[8 * j:8 * j + 8, h * NBF:(h + 1) * NBF]
        recv[step, me] = sendbuf[step, me]
        for k in range(1, DEVS):
            to, where = peer(k)
            pltpu.make_async_remote_copy(
                src_ref=sendbuf.at[step, to], dst_ref=recv.at[step, me],
                send_sem=send_sem, recv_sem=recv_sem.at[step],
                device_id=where, device_id_type=MESH).start()

        @pl.when(step + SLOTS < STEPS)
        def _():
            fetch(step + SLOTS, slot).start()

        return carry

    lax.fori_loop(0, STEPS, step_body, 0)

    def arrived(step, carry):
        view = recv.at[step, pl.ds(0, DEVS - 1)]
        pltpu.make_async_copy(view, view, recv_sem.at[step]).wait()
        return carry

    lax.fori_loop(0, STEPS, arrived, 0)
    sums = []
    for r in range(2):
        part = recv[:, COLS * r] + recv[:, COLS * r + 1]
        part += recv[:, COLS * r + 2] + recv[:, COLS * r + 3]
        sums.append(part.reshape(STEPS * 8, NBF))
    even = jnp.concatenate(sums, axis=0)
    both = jnp.concatenate([even, pltpu.roll(even, 64, 1)], axis=0)
    high = both.astype(BF16)
    rest = both - high.astype(F32)
    mid = rest.astype(BF16)
    low = (rest - mid.astype(F32)).astype(BF16)
    left = cvx[...]
    total = dot(left, high) + dot(left, mid) + dot(left, low)
    for i in range(OCC):
        out_ref[i] = total[i * VIRT:(i + 1) * VIRT, :HALF]

    sent = sendbuf.at[:, pl.ds(0, DEVS - 1)]
    pltpu.make_async_copy(sent, sent, send_sem).wait()


def solution(mesh):
    def local_block(ao_blk, c_occ, c_virt):
        hbm = pl.BlockSpec(memory_space=pltpu.HBM)
        return pl.pallas_call(
            kernel,
            out_shape=jax.ShapeDtypeStruct((OCC, VIRT, HALF), F32),
            in_specs=[hbm] * 3,
            out_specs=pl.BlockSpec(memory_space=pltpu.VMEM),
            scratch_shapes=[
                pltpu.VMEM((SLOTS, ROWS_P, TILE_Q, NBF, NBF), BF16),
                pltpu.VMEM((NBF, OCC), BF16),
                pltpu.VMEM((NBF, VIRT), BF16),
                pltpu.VMEM((16, 256), BF16),
                pltpu.VMEM((256, 256), BF16),
                pltpu.VMEM((32, 256), BF16),
                pltpu.VMEM((OCC * VIRT, 512), BF16),
                pltpu.VMEM((256, 256), BF16),
                pltpu.VMEM((STEPS, DEVS, 8, NBF), F32),
                pltpu.VMEM((STEPS, DEVS, 8, NBF), F32),
                pltpu.SemaphoreType.DMA((SLOTS,)),
                pltpu.SemaphoreType.DMA((2,)),
                pltpu.SemaphoreType.DMA,
                pltpu.SemaphoreType.DMA((STEPS,)),
            ],
            compiler_params=pltpu.CompilerParams(
                collective_id=0, has_side_effects=True, vmem_limit_bytes=48 * 1024 * 1024),
        )(ao_blk, c_occ, c_virt)

    return jax.shard_map(
        local_block, mesh=mesh,
        in_specs=(P(("frag", "dev"), "dev2", None, None), P("frag", None), P("frag", None)),
        out_specs=P("frag", None, ("dev2", "dev")),
        check_vma=False)
```

time: 104 us -> 30.7 us (0.30)
  blocking collectives: 53.4 us -> 0 us
  Pallas kernels: 0 us -> 28.1 us
  matrix products: 26.7 us -> 0 us
  local copies, waits for them, and re-layouts: 23.8 us -> 2.42 us
    all_to_all x2 -> x0, blocking collectives: 53.4 us -> none  [the longest x1 27.2 us: local_block(): q_whole = lax.all_to_all(half_blk, 'dev2', 2, 1, tiled=True)]
    pallas_call x0 -> x1, Pallas kernels: none -> 28.1 us  [local_block(): pl.pallas_call(kernel, out_shape=jax.ShapeDtypeStruct((OCC, VIRT, HALF),...]
    dot_general x4 -> x0, matrix products: 26.7 us -> none  [the longest x1 23.5 us: local_block(): jnp.einsum('pqrs,rj->pqsj', ao_blk, c_occ, preferred_element_type=jnp.flo...]
    unnamed x6 -> x2, local copies, waits for them, and re-layouts: 9.49 us -> 1.66 us
    all_to_all x3 -> x0, local copies, waits for them, and re-layouts: 7.34 us -> none  [the longest x2 6.63 us: local_block(): q_whole = lax.all_to_all(half_blk, 'dev2', 2, 1, tiled=True)]
    reshape x1 -> x0, local copies, waits for them, and re-layouts: 6.95 us -> none  [local_block(): half_blk.reshape(ao_blk.shape[0], ao_blk.shape[1], occ_num * virt_num)]
where the time goes in v1:
time: 30.7 us; the launch traced here: 30.6 us
  Pallas kernels  28.1 us (92%)
  local copies, waits for them, and re-layouts  2.42 us (8%)
    pallas_call x1, Pallas kernels, local_block(): pl.pallas_call(kernel, out_shape=jax.ShapeDtypeStruct((OCC, VIRT, HALF),...  28.1 us
    unnamed x2, local copies, waits for them, and re-layouts  1.66 us
    pallas_call x1, local copies, waits for them, and re-layouts, local_block(): pl.pallas_call(kernel, out_shape=jax.ShapeDtypeStruct((OCC, VIRT, HALF),...  0.76 us

profile of v1, /device:TPU:0, one launch (start us, length us, event | category | flops | bytes accessed | tf_op | source)
XLA Modules:
  0.0 30.6 jit_solution(17084191230469825716)
XLA Ops:
  0.0 0.8 %copy.4.co_hbm = bf16[128,4]{1,0:T(8,128)(2,1)S(1)} copy(bf16[128,4]{0,1:T(4,128)(2,1)} %param.4) | data formatting | bytes 2048 | tf_op args[1]
  0.8 0.9 %copy.5.cv_hbm = bf16[128,112]{1,0:T(8,128)(2,1)S(1)} copy(bf16[128,112]{0,1:T(8,128)(2,1)} %param.5) | data formatting | bytes 57344 | tf_op args[2]
  1.7 28.1 %shard_map.37 = f32[4,112,56]{2,1,0:T(8,128)S(1)} custom-call(bf16[32,64,128,128]{3,2,1,0:T(8,128)(2,1)} %a_hbm.1, bf16[128,4]{1,0:T(8,128)(2,1)S(1)} %copy.4.co_hbm, bf16[128,112]{1,0:T(8,128)(2,1)S(1)} %copy.5.cv_hbm), custom_call_target="tpu_custom_call" | custom-call | tf_op jit(solution)/shard_map/pallas_call | solution.py:163
  29.8 0.8 %copy.6 = f32[4,112,56]{1,2,0:T(8,128)} copy(f32[4,112,56]{2,1,0:T(8,128)S(1)} %shard_map.37) | data formatting | bytes 200704 | tf_op jit(solution)/shard_map/pallas_call | solution.py:163

commit v2 on v1

--- a/solution.py
+++ b/solution.py
@@ -44,7 +44,7 @@
     return lax.dot_general(a, b, (((0,), (0,)), ((), ())), preferred_element_type=F32)
 
 
-def kernel(a_hbm, co_hbm, cv_hbm, out_ref, abuf, co_ref, cv_ref, lhs1, cv2, w2, cvx, t1, sendbuf, recv,
+def kernel(a_hbm, co_hbm, cv_hbm, recv, cvx, abuf, co_ref, cv_ref, lhs1, cv2, w2, t1, sendbuf,
            a_sem, c_sem, send_sem, recv_sem):
     row, col = lax.axis_index("dev2"), lax.axis_index("dev")
     me = row * COLS + col
@@ -71,29 +71,28 @@
     cv_copy.wait()
     co, cv = co_ref[...], cv_ref[...]
 
-    r16, c4 = iota((16, OCC), 0), iota((16, OCC), 1)
-    co_t = dot_nt(one_hot(r16 % OCC == c4), co)
+    co_t = dot(one_hot(iota((16, OCC), 0) % OCC == iota((16, OCC), 1)), co)
     r16 = iota((16, NBF), 0)
     lhs1[...] = jnp.concatenate(
         [jnp.where(r16 // OCC == k, co_t, 0.0) for k in range(2)], axis=1).astype(BF16)
 
-    co_i = dot_nt(one_hot(iota((32, OCC), 0) % OCC == iota((32, OCC), 1)), co).astype(BF16)
+    co_i = dot(one_hot(iota((32, OCC), 0) % OCC == iota((32, OCC), 1)), co).astype(BF16)
     r, c = iota((NBF, 256), 0), iota((NBF, 256), 1)
     spread = dot(co_i, one_hot(r == col * ROWS_P + (c % NBF) // OCC))
     r, c = iota((32, 256), 0), iota((32, 256), 1)
     w2[...] = jnp.where(((r // OCC) % 2 == c // NBF) & (r // 8 == c % OCC), spread, 0.0).astype(BF16)
 
     b, c = iota((VIRT, 256), 0), iota((VIRT, 256), 1)
-    halves = dot(cv, one_hot((b == (c // NBF) * HALF + c % 64) & (c % 64 < HALF)))
+    halves = dot_tn(cv, one_hot((b == (c // NBF) * HALF + c % 64) & (c % 64 < HALF)))
     c = iota((NBF, 256), 1)
     for par in range(2):
         cv2[par * NBF:(par + 1) * NBF, :] = jnp.where((c // 64) % 2 == par, halves, 0.0).astype(BF16)
 
-    q, c = iota((NBF, 512), 0), iota((NBF, 512), 1)
-    rows = dot_tn(cv, one_hot(q == ((c % 256) // OCC) * 2 + c // 256))
-    c = iota((VIRT, 512), 1)
+    wide = jnp.concatenate([cv, jnp.zeros((NBF - VIRT, NBF), BF16)], axis=0)
+    r, q = iota((512, NBF), 0), iota((512, NBF), 1)
+    rows = dot_nt(one_hot(q == ((r % 256) // OCC) * 2 + r // 256), wide)
     for i in range(OCC):
-        cvx[i * VIRT:(i + 1) * VIRT, :] = jnp.where(c % OCC == i, rows, 0.0).astype(BF16)
+        cvx[:, i * NBF:(i + 1) * NBF] = jnp.where(r % OCC == i, rows, 0.0).astype(BF16)
 
     pl.semaphore_wait(barrier, DEVS - 1)
 
@@ -137,44 +136,48 @@
         return carry
 
     lax.fori_loop(0, STEPS, arrived, 0)
+    sent = sendbuf.at[:, pl.ds(0, DEVS - 1)]
+    pltpu.make_async_copy(sent, sent, send_sem).wait()
+
+
+def finish(recv, cvx, out_ref):
     sums = []
     for r in range(2):
         part = recv[:, COLS * r] + recv[:, COLS * r + 1]
         part += recv[:, COLS * r + 2] + recv[:, COLS * r + 3]
-        sums.append(part.reshape(STEPS * 8, NBF))
-    even = jnp.concatenate(sums, axis=0)
-    both = jnp.concatenate([even, pltpu.roll(even, 64, 1)], axis=0)
+        sums.append(part.reshape(STEPS * 8, NBF).T)
+    half = jnp.concatenate(sums, axis=1)
+    both = jnp.concatenate([half[:64], half[64:]], axis=1)
     high = both.astype(BF16)
     rest = both - high.astype(F32)
     mid = rest.astype(BF16)
     low = (rest - mid.astype(F32)).astype(BF16)
-    left = cvx[...]
-    total = dot(left, high) + dot(left, mid) + dot(left, low)
+    right = cvx[...]
+    total = dot(high, right) + dot(mid, right) + dot(low, right)
     for i in range(OCC):
-        out_ref[i] = total[i * VIRT:(i + 1) * VIRT, :HALF]
-
-    sent = sendbuf.at[:, pl.ds(0, DEVS - 1)]
-    pltpu.make_async_copy(sent, sent, send_sem).wait()
+        out_ref[i] = total[:HALF, i * NBF:i * NBF + VIRT]
 
 
 def solution(mesh):
     def local_block(ao_blk, c_occ, c_virt):
         hbm = pl.BlockSpec(memory_space=pltpu.HBM)
-        return pl.pallas_call(
+        vmem = pl.BlockSpec(memory_space=pltpu.VMEM)
+        recv, cvx = pl.pallas_call(
             kernel,
-            out_shape=jax.ShapeDtypeStruct((OCC, VIRT, HALF), F32),
+            out_shape=[
+                jax.ShapeDtypeStruct((STEPS, DEVS, 8, NBF), F32),
+                jax.ShapeDtypeStruct((512, 512), BF16),
+            ],
             in_specs=[hbm] * 3,
-            out_specs=pl.BlockSpec(memory_space=pltpu.VMEM),
+            out_specs=[vmem] * 2,
             scratch_shapes=[
                 pltpu.VMEM((SLOTS, ROWS_P, TILE_Q, NBF, NBF), BF16),
-                pltpu.VMEM((NBF, OCC), BF16),
-                pltpu.VMEM((NBF, VIRT), BF16),
+                pltpu.VMEM((OCC, NBF), BF16),
+                pltpu.VMEM((VIRT, NBF), BF16),
                 pltpu.VMEM((16, 256), BF16),
                 pltpu.VMEM((256, 256), BF16),
                 pltpu.VMEM((32, 256), BF16),
-                pltpu.VMEM((OCC * VIRT, 512), BF16),
                 pltpu.VMEM((256, 256), BF16),
-                pltpu.VMEM((STEPS, DEVS, 8, NBF), F32),
                 pltpu.VMEM((STEPS, DEVS, 8, NBF), F32),
                 pltpu.SemaphoreType.DMA((SLOTS,)),
                 pltpu.SemaphoreType.DMA((2,)),
@@ -183,7 +186,16 @@
             ],
             compiler_params=pltpu.CompilerParams(
                 collective_id=0, has_side_effects=True, vmem_limit_bytes=48 * 1024 * 1024),
-        )(ao_blk, c_occ, c_virt)
+        )(ao_blk, pltpu.with_memory_space_constraint(c_occ.T, pltpu.HBM),
+          pltpu.with_memory_space_constraint(c_virt.T, pltpu.HBM))
+        out = pl.pallas_call(
+            finish,
+            out_shape=jax.ShapeDtypeStruct((OCC, HALF, VIRT), F32),
+            in_specs=[vmem] * 2,
+            out_specs=vmem,
+            compiler_params=pltpu.CompilerParams(vmem_limit_bytes=8 * 1024 * 1024),
+        )(recv, cvx)
+        return jnp.swapaxes(out, 1, 2)
 
     return jax.shard_map(
         local_block, mesh=mesh,

time: 30.7 us -> 32 us (1.042)
  Pallas kernels: 28.1 us -> 31.9 us
  local copies, waits for them, and re-layouts: 2.42 us -> 0 us
    pallas_call x1 -> x2, Pallas kernels: 28.1 us -> 31.9 us  [the longest x1 30.8 us: local_block(): pl.pallas_call(kernel, out_shape=[jax.ShapeDtypeStruct((STEPS, DEVS, 8, N...]
    unnamed x2 -> x0, local copies, waits for them, and re-layouts: 1.66 us -> none
    pallas_call x1 -> x0, local copies, waits for them, and re-layouts: 0.76 us -> none  [local_block(): pl.pallas_call(kernel, out_shape=jax.ShapeDtypeStruct((OCC, VIRT, HALF),...]
where the time goes in v2:
time: 32 us; the launch traced here: 31.9 us
  Pallas kernels  31.9 us (100%)
    pallas_call x1, Pallas kernels, local_block(): pl.pallas_call(kernel, out_shape=[jax.ShapeDtypeStruct((STEPS, DEVS, 8, N...  30.8 us
    pallas_call x1, Pallas kernels, local_block(): pl.pallas_call(finish, out_shape=jax.ShapeDtypeStruct((OCC, HALF, VIRT),...  1.08 us

profile of v2, /device:TPU:0, one launch (start us, length us, event | category | flops | bytes accessed | tf_op | source)
XLA Modules:
  0.0 31.9 jit_solution(3621627491917559603)
XLA Ops:
  0.0 30.8 %shard_map.37 = (f32[16,8,8,128]{3,2,1,0:T(8,128)S(1)}, bf16[512,512]{1,0:T(8,128)(2,1)S(1)}) custom-call(bf16[32,64,128,128]{3,2,1,0:T(8,128)(2,1)} %a_hbm.1, bf16[4,128]{1,0:T(4,128)(2,1)} %bitcast.4, bf16[112,128]{1,0:T(8,128)(2,1)} %bitcast.3), custom_call_target="tpu_custom_call" | custom-call | tf_op jit(solution)/shard_map/pallas_call | solution.py:165
  30.8 1.1 %shard_map.38 = f32[4,56,112]{2,1,0:T(8,128)} custom-call(f32[16,8,8,128]{3,2,1,0:T(8,128)S(1)} %get-tuple-element.7.recv, bf16[512,512]{1,0:T(8,128)(2,1)S(1)} %get-tuple-element.8.cvx), custom_call_target="tpu_custom_call" | custom-call | tf_op jit(solution)/shard_map/pallas_call | solution.py:191

commit v3 on v2

--- a/solution.py
+++ b/solution.py
@@ -57,7 +57,7 @@
     co_copy.start()
     cv_copy.start()
     for s in range(SLOTS):
-        fetch(s, s).start()
+        fetch(s, s).start(priority=1)
 
     def peer(k):
         to = lax.rem(me + k, DEVS)
@@ -124,7 +124,7 @@
 
         @pl.when(step + SLOTS < STEPS)
         def _():
-            fetch(step + SLOTS, slot).start()
+            fetch(step + SLOTS, slot).start(priority=1)
 
         return carry
 

time: 32 us -> 28.7 us (0.90)
  Pallas kernels: 31.9 us -> 28.6 us
    pallas_call x1, Pallas kernels: 30.8 us -> 27.5 us  [local_block(): pl.pallas_call(kernel, out_shape=[jax.ShapeDtypeStruct((STEPS, DEVS, 8, N...]
where the time goes in v3:
time: 28.7 us; the launch traced here: 28.6 us
  Pallas kernels  28.6 us (100%)
    pallas_call x1, Pallas kernels, local_block(): pl.pallas_call(kernel, out_shape=[jax.ShapeDtypeStruct((STEPS, DEVS, 8, N...  27.5 us
    pallas_call x1, Pallas kernels, local_block(): pl.pallas_call(finish, out_shape=jax.ShapeDtypeStruct((OCC, HALF, VIRT),...  1.08 us

profile of v3, /device:TPU:0, one launch (start us, length us, event | category | flops | bytes accessed | tf_op | source)
XLA Modules:
  0.0 28.6 jit_solution(17875663673969843316)
XLA Ops:
  0.0 27.5 %shard_map.37 = (f32[16,8,8,128]{3,2,1,0:T(8,128)S(1)}, bf16[512,512]{1,0:T(8,128)(2,1)S(1)}) custom-call(bf16[32,64,128,128]{3,2,1,0:T(8,128)(2,1)} %a_hbm.1, bf16[4,128]{1,0:T(4,128)(2,1)} %bitcast.4, bf16[112,128]{1,0:T(8,128)(2,1)} %bitcast.3), custom_call_target="tpu_custom_call" | custom-call | tf_op jit(solution)/shard_map/pallas_call | solution.py:165
  27.5 1.1 %shard_map.38 = f32[4,56,112]{2,1,0:T(8,128)} custom-call(f32[16,8,8,128]{3,2,1,0:T(8,128)S(1)} %get-tuple-element.7.recv, bf16[512,512]{1,0:T(8,128)(2,1)S(1)} %get-tuple-element.8.cvx), custom_call_target="tpu_custom_call" | custom-call | tf_op jit(solution)/shard_map/pallas_call | solution.py:191

commit v4 on v3

v4 whole, which is shorter than its diff:
```python
import functools

import jax
import jax.numpy as jnp
from jax import lax
from jax.experimental import pallas as pl
from jax.experimental.pallas import tpu as pltpu
from jax.sharding import PartitionSpec as P

MESH = pl.DeviceIdType.MESH
F32 = jnp.float32
BF16 = jnp.bfloat16

ROWS_P = 32
ROWS_Q = 64
NBF = 128
OCC = 4
VIRT = 112
HALF = VIRT // 2
TILE_Q = 4
STEPS = ROWS_Q // TILE_Q
SLOTS = 8
DEVS = 8
COLS = 4
PIECES = ((14, 0, 16), (14, 16, 16), (15, 0, 8), (15, 8, 8), (15, 16, 8), (15, 24, 8))
LAST = STEPS - 1
LOOPED = STEPS - 2


def iota(shape, dim):
    return lax.broadcasted_iota(jnp.int32, shape, dim)


def one_hot(cond):
    return jnp.where(cond, 1.0, 0.0).astype(BF16)


def dot(a, b):
    return jnp.dot(a, b, preferred_element_type=F32)


def dot_nt(a, b):
    return lax.dot_general(a, b, (((1,), (1,)), ((), ())), preferred_element_type=F32)


def dot_tn(a, b):
    return lax.dot_general(a, b, (((0,), (0,)), ((), ())), preferred_element_type=F32)


def split(x):
    high = x.astype(BF16)
    rest = x - high.astype(F32)
    mid = rest.astype(BF16)
    return high, mid, (rest - mid.astype(F32)).astype(BF16)


def kernel(*refs):
    pl.run_scoped(
        functools.partial(body, *refs),
        pltpu.SemaphoreType.DMA((SLOTS,)),
        pltpu.SemaphoreType.DMA((len(PIECES),)),
        pltpu.SemaphoreType.DMA((2,)),
    )


def body(a_hbm, co_hbm, cv_hbm, recv, base, cvd, abuf, co_ref, cv_ref, lhs1, cv2, w2, w2a, w2b, cvx, t1, sendbuf,
         send_sem, recv_sem, a_sem, l_sem, c_sem):
    row, col = lax.axis_index("dev2"), lax.axis_index("dev")
    me = row * COLS + col

    def fetch(step, slot):
        return pltpu.make_async_copy(a_hbm.at[:, pl.ds(step * TILE_Q, TILE_Q)], abuf.at[slot], a_sem.at[slot])

    def fetch_piece(n):
        step, first, count = PIECES[n]
        part = pl.ds(first, count)
        return pltpu.make_async_copy(
            a_hbm.at[part, pl.ds(step * TILE_Q, TILE_Q)], abuf.at[step % SLOTS, part], l_sem.at[n])

    co_copy = pltpu.make_async_copy(co_hbm, co_ref, c_sem.at[0])
    cv_copy = pltpu.make_async_copy(cv_hbm, cv_ref, c_sem.at[1])
    co_copy.start()
    cv_copy.start()
    for s in range(SLOTS):
        fetch(s, s).start(priority=1)

    x, core = col // 2, lax.rem(col, 2)
    far_row, far_x = 1 - row, 1 - x
    peers = [(far_row, 2 * far_x), (far_row, 2 * far_x + 1), (far_row, 2 * x), (far_row, 2 * x + 1),
             (row, 2 * far_x), (row, 2 * far_x + 1), (row, 2 * x + 1 - core)]

    barrier = pltpu.get_barrier_semaphore()
    for r, c in peers:
        pl.semaphore_signal(barrier, inc=1, device_id={"dev2": r, "dev": c}, device_id_type=MESH)

    co_copy.wait()
    cv_copy.wait()
    co, cv = co_ref[...], cv_ref[...]

    co_t = dot(one_hot(iota((16, OCC), 0) % OCC == iota((16, OCC), 1)), co)
    r16 = iota((16, NBF), 0)
    lhs1[...] = jnp.concatenate(
        [jnp.where(r16 // OCC == k, co_t, 0.0) for k in range(2)], axis=1).astype(BF16)

    co_i = dot(one_hot(iota((32, OCC), 0) % OCC == iota((32, OCC), 1)), co).astype(BF16)

    def spread(groups):
        width = sum(2 * count * OCC for _, count in groups)
        r, c = iota((NBF, width), 0), iota((NBF, width), 1)
        c32, r32 = iota((32, width), 1), iota((32, width), 0)
        pick, qp, at = r < 0, c32 < 0, 0
        for first, count in groups:
            half = count * OCC
            pick |= (r == col * ROWS_P + first + (c - at) % half // OCC) & (c >= at) & (c < at + 2 * half)
            qp |= (r32 // OCC % 2 == (c32 - at) // half) & (c32 >= at) & (c32 < at + 2 * half)
            at += 2 * half
        placed = dot(co_i, one_hot(pick))
        return jnp.where(qp & (r32 // 8 == c32 % OCC), placed, 0.0).astype(BF16)

    w2[...] = spread([(0, ROWS_P)])
    w2a[...] = spread([(0, 16)])
    w2b[...] = spread([(16, 8), (24, 8)])

    b, c = iota((VIRT, 256), 0), iota((VIRT, 256), 1)
    halves = dot_tn(cv, one_hot((b == (c // NBF) * HALF + c % 64) & (c % 64 < HALF)))
    c = iota((NBF, 256), 1)
    for par in range(2):
        cv2[par * NBF:(par + 1) * NBF, :] = jnp.where((c // 64) % 2 == par, halves, 0.0).astype(BF16)

    wide = jnp.concatenate([cv, jnp.zeros((NBF - VIRT, NBF), BF16)], axis=0)
    r, q = iota((512, NBF), 0), iota((512, NBF), 1)
    rows = dot_nt(one_hot(q == ((r % 256) // OCC) * 2 + r // 256), wide)
    for i in range(OCC):
        cvx[:, i * NBF:(i + 1) * NBF] = jnp.where(r % OCC == i, rows, 0.0).astype(BF16)
    r, q = iota((256, NBF), 0), iota((256, NBF), 1)
    at = (r // 8) % 2 * ROWS_Q + LAST * TILE_Q + (r % 8) // OCC * 2 + r // NBF
    rows = dot_nt(one_hot((q == at) & (r % NBF < 48)), wide)
    for i in range(OCC):
        cvd[:, i * NBF:(i + 1) * NBF] = jnp.where(r % OCC == i, rows, 0.0).astype(BF16)

    pl.semaphore_wait(barrier, DEVS - 1)

    def contract_r(slot, blocks):
        left = lhs1[...]
        for qp, pb, at in blocks:
            parts = []
            for p0 in (pb, pb + 2):
                rhs = jnp.concatenate(
                    [abuf[slot, p0:p0 + 2, 2 * qp + par].reshape(256, NBF) for par in range(2)], axis=1)
                parts.append(dot(left, rhs)[:8])
            t1[at:at + 16, :] = jnp.concatenate(parts, axis=0).astype(BF16)

    def contract_s(t_one):
        return dot(t_one, cv2[...]).astype(BF16)

    def pack(step, e_part):
        for j in range(OCC):
            for h in range(2):
                sendbuf[step, 2 * j + h] = e_part[8 * j:8 * j + 8, h * NBF:(h + 1) * NBF]

    def send(step, sem):
        for r, c in peers:
            pltpu.make_async_remote_copy(
                src_ref=sendbuf.at[step, r * COLS + c], dst_ref=recv.at[step, me],
                send_sem=send_sem, recv_sem=recv_sem.at[sem],
                device_id={"dev2": r, "dev": c}, device_id_type=MESH).start()
        recv[step, me] = sendbuf[step, me]

    def blocks(first, count, at):
        return [(qp, first + pb, at + qp * count * OCC + pb * OCC) for qp in range(2) for pb in range(0, count, 4)]

    whole = blocks(0, ROWS_P, 0)
    upper = [b for b in whole if b[1] < 16]
    lower = [b for b in whole if b[1] >= 16]

    def refill(step, slot):
        @pl.when(step + SLOTS < LOOPED)
        def _():
            fetch(step + SLOTS, slot).start(priority=1)

        for n in range(len(PIECES)):
            @pl.when(step + SLOTS == PIECES[n][0])
            def _():
                fetch_piece(n).start(priority=1)

    def beside(step, slot, mine):
        half = contract_s(t1[...])
        contract_r(slot, mine[:4])
        e_part = dot(w2[...], half)
        contract_r(slot, mine[4:])
        pack(step - 1, e_part)
        send(step - 1, 0)

    def step_body(step, carry):
        slot = lax.rem(step, SLOTS)
        fetch(step, slot).wait()
        beside(step, slot, whole)
        refill(step, slot)
        return carry

    fetch(0, 0).wait()
    contract_r(0, whole)
    refill(0, 0)
    lax.fori_loop(1, LOOPED, step_body, 0)

    slot = LOOPED % SLOTS
    fetch_piece(0).wait()
    beside(LOOPED, slot, upper)
    fetch_piece(1).wait()
    contract_r(slot, lower)
    slot = LAST % SLOTS
    fetch_piece(2).wait()
    beside(LAST, slot, [b for b in blocks(0, 16, 0) if b[1] < 8])
    fetch_piece(3).wait()
    contract_r(slot, [b for b in blocks(0, 16, 0) if b[1] >= 8])
    fetch_piece(4).wait()
    half = contract_s(t1[:128, :])
    contract_r(slot, blocks(16, 8, 128))
    e_part = dot(w2a[...], half)
    fetch_piece(5).wait()
    contract_r(slot, blocks(24, 8, 192))
    half = jnp.concatenate([contract_s(t1[128:192, :]), contract_s(t1[192:, :])], axis=0)
    e_part += dot(w2b[...], half)
    pack(LAST, e_part)
    send(LAST, 1)

    def arrived(view, sem):
        pltpu.make_async_copy(view, view, recv_sem.at[sem]).wait()

    arrived(recv.at[pl.ds(0, LAST), pl.ds(0, DEVS - 1)], 0)
    sums = []
    for r in range(2):
        part = recv[:LAST, COLS * r] + recv[:LAST, COLS * r + 1]
        part += recv[:LAST, COLS * r + 2] + recv[:LAST, COLS * r + 3]
        part = jnp.concatenate([part.reshape(LAST * 8, NBF), jnp.zeros((8, NBF), F32)], axis=0)
        sums.append(part.T)
    half = jnp.concatenate(sums, axis=1)
    high, mid, low = split(jnp.concatenate([half[:64], half[64:]], axis=1))
    right = cvx[...]
    base[...] = dot(high, right) + dot(mid, right) + dot(low, right)

    arrived(recv.at[LAST, pl.ds(0, DEVS - 1)], 1)
    sent = sendbuf.at[:, pl.ds(0, DEVS - 1)]
    pltpu.make_async_copy(sent, sent, send_sem).wait()


def finish(recv, base, cvd, out_ref):
    sums = []
    for r in range(2):
        part = recv[STEPS - 1, COLS * r] + recv[STEPS - 1, COLS * r + 1]
        sums.append(part + (recv[STEPS - 1, COLS * r + 2] + recv[STEPS - 1, COLS * r + 3]))
    parts = [x.astype(F32) for x in split(jnp.concatenate(sums, axis=0))]
    turned = jnp.concatenate(parts + [jnp.zeros((NBF - 48, NBF), F32)], axis=0).T.astype(BF16)
    total = base[...] + dot(jnp.concatenate([turned[:64], turned[64:]], axis=1), cvd[...])
    for i in range(OCC):
        out_ref[i] = total[:HALF, i * NBF:i * NBF + VIRT]


def solution(mesh):
    def local_block(ao_blk, c_occ, c_virt):
        hbm = pl.BlockSpec(memory_space=pltpu.HBM)
        vmem = pl.BlockSpec(memory_space=pltpu.VMEM)
        recv, base, cvd = pl.pallas_call(
            kernel,
            out_shape=[
                jax.ShapeDtypeStruct((STEPS, DEVS, 8, NBF), F32),
                jax.ShapeDtypeStruct((64, 512), F32),
                jax.ShapeDtypeStruct((256, 512), BF16),
            ],
            in_specs=[hbm] * 3,
            out_specs=[vmem] * 3,
            scratch_shapes=[
                pltpu.VMEM((SLOTS, ROWS_P, TILE_Q, NBF, NBF), BF16),
                pltpu.VMEM((OCC, NBF), BF16),
                pltpu.VMEM((VIRT, NBF), BF16),
                pltpu.VMEM((16, 256), BF16),
                pltpu.VMEM((256, 256), BF16),
                pltpu.VMEM((32, 256), BF16),
                pltpu.VMEM((32, NBF), BF16),
                pltpu.VMEM((32, NBF), BF16),
                pltpu.VMEM((512, 512), BF16),
                pltpu.VMEM((256, 256), BF16),
                pltpu.VMEM((STEPS, DEVS, 8, NBF), F32),
                pltpu.SemaphoreType.DMA,
                pltpu.SemaphoreType.DMA((2,)),
            ],
            compiler_params=pltpu.CompilerParams(
                collective_id=0, has_side_effects=True, vmem_limit_bytes=48 * 1024 * 1024),
        )(ao_blk, pltpu.with_memory_space_constraint(c_occ.T, pltpu.HBM),
          pltpu.with_memory_space_constraint(c_virt.T, pltpu.HBM))
        out = pl.pallas_call(
            finish,
            out_shape=jax.ShapeDtypeStruct((OCC, HALF, VIRT), F32),
            in_specs=[vmem] * 3,
            out_specs=vmem,
            compiler_params=pltpu.CompilerParams(vmem_limit_bytes=8 * 1024 * 1024),
        )(recv, base, cvd)
        return jnp.swapaxes(out, 1, 2)

    return jax.shard_map(
        local_block, mesh=mesh,
        in_specs=(P(("frag", "dev"), "dev2", None, None), P("frag", None), P("frag", None)),
        out_specs=P("frag", None, ("dev2", "dev")),
        check_vma=False)
```

time: 28.7 us -> 28 us (0.976)
  Pallas kernels: 28.6 us -> 27.9 us
    pallas_call x1, Pallas kernels: 27.5 us -> 27 us  [local_block(): pl.pallas_call(kernel, out_shape=[jax.ShapeDtypeStruct((STEPS, DEVS, 8, N...]
where the time goes in v4:
time: 28 us; the launch traced here: 27.9 us
  Pallas kernels  27.9 us (100%)
    pallas_call x1, Pallas kernels, local_block(): pl.pallas_call(kernel, out_shape=[jax.ShapeDtypeStruct((STEPS, DEVS, 8, N...  27 us
    pallas_call x1, Pallas kernels, local_block(): pl.pallas_call(finish, out_shape=jax.ShapeDtypeStruct((OCC, HALF, VIRT),...  0.88 us

profile of v4, /device:TPU:0, one launch (start us, length us, event | category | flops | bytes accessed | tf_op | source)
XLA Modules:
  0.0 27.9 jit_solution(3008313198467644116)
XLA Ops:
  0.0 27.0 %shard_map.37 = (f32[16,8,8,128]{3,2,1,0:T(8,128)S(1)}, f32[64,512]{1,0:T(8,128)S(1)}, bf16[256,512]{1,0:T(8,128)(2,1)S(1)}) custom-call(bf16[32,64,128,128]{3,2,1,0:T(8,128)(2,1)} %refs_0_.1, bf16[4,128]{1,0:T(4,128)(2,1)} %bitcast.4, bf16[112,128]{1,0:T(8,128)(2,1)} %bitcast.3), custom_call_target="tpu_custom_call" | custom-call | tf_op jit(solution)/shard_map/pallas_call | solution.py:263
  27.0 0.9 %shard_map.38 = f32[4,56,112]{2,1,0:T(8,128)} custom-call(f32[16,8,8,128]{3,2,1,0:T(8,128)S(1)} %get-tuple-element.8.recv, f32[64,512]{1,0:T(8,128)S(1)} %get-tuple-element.9.base, bf16[256,512]{1,0:T(8,128)(2,1)S(1)} %get-tuple-element.10.cvd), custom_call_target="tpu_custom_call" | custom-call | tf_op jit(solution)/shard_map/pallas_call | solution.py:291

commit v5 on v4

--- a/solution.py
+++ b/solution.py
@@ -19,7 +19,9 @@
 HALF = VIRT // 2
 TILE_Q = 4
 STEPS = ROWS_Q // TILE_Q
-SLOTS = 8
+SLOTS = 6
+GIVEN = 2
+EVERY = 6
 DEVS = 8
 COLS = 4
 PIECES = ((14, 0, 16), (14, 16, 16), (15, 0, 8), (15, 8, 8), (15, 16, 8), (15, 24, 8))
@@ -64,25 +66,28 @@
 
 
 def body(a_hbm, co_hbm, cv_hbm, recv, base, cvd, abuf, co_ref, cv_ref, lhs1, cv2, w2, w2a, w2b, cvx, t1, sendbuf,
-         send_sem, recv_sem, a_sem, l_sem, c_sem):
+         send_sem, recv_sem, give_sem, take_sem, a_sem, l_sem, c_sem):
     row, col = lax.axis_index("dev2"), lax.axis_index("dev")
     me = row * COLS + col
 
-    def fetch(step, slot):
-        return pltpu.make_async_copy(a_hbm.at[:, pl.ds(step * TILE_Q, TILE_Q)], abuf.at[slot], a_sem.at[slot])
+    def slot_of(tile):
+        return lax.rem(tile - GIVEN, SLOTS)
+
+    def fetch(tile, slot):
+        return pltpu.make_async_copy(a_hbm.at[:, pl.ds(tile * TILE_Q, TILE_Q)], abuf.at[slot], a_sem.at[slot])
 
     def fetch_piece(n):
-        step, first, count = PIECES[n]
+        tile, first, count = PIECES[n]
         part = pl.ds(first, count)
         return pltpu.make_async_copy(
-            a_hbm.at[part, pl.ds(step * TILE_Q, TILE_Q)], abuf.at[step % SLOTS, part], l_sem.at[n])
+            a_hbm.at[part, pl.ds(tile * TILE_Q, TILE_Q)], abuf.at[(tile - GIVEN) % SLOTS, part], l_sem.at[n])
 
     co_copy = pltpu.make_async_copy(co_hbm, co_ref, c_sem.at[0])
     cv_copy = pltpu.make_async_copy(cv_hbm, cv_ref, c_sem.at[1])
     co_copy.start()
     cv_copy.start()
     for s in range(SLOTS):
-        fetch(s, s).start(priority=1)
+        fetch(GIVEN + s, s).start(priority=1)
 
     x, core = col // 2, lax.rem(col, 2)
     far_row, far_x = 1 - row, 1 - x
@@ -92,6 +97,16 @@
     barrier = pltpu.get_barrier_semaphore()
     for r, c in peers:
         pl.semaphore_signal(barrier, inc=1, device_id={"dev2": r, "dev": c}, device_id_type=MESH)
+    pl.semaphore_wait(barrier, DEVS - 1)
+
+    other = 2 * x + 1 - core
+    gifts = []
+    for k in range(GIVEN):
+        gifts.append(pltpu.make_async_remote_copy(
+            src_ref=a_hbm.at[:, pl.ds(k * TILE_Q, TILE_Q)], dst_ref=abuf.at[SLOTS + k],
+            send_sem=give_sem.at[k], recv_sem=take_sem.at[k],
+            device_id={"dev2": row, "dev": other}, device_id_type=MESH))
+        gifts[k].start()
 
     co_copy.wait()
     cv_copy.wait()
@@ -104,22 +119,23 @@
 
     co_i = dot(one_hot(iota((32, OCC), 0) % OCC == iota((32, OCC), 1)), co).astype(BF16)
 
-    def spread(groups):
+    def spread(dev, groups):
         width = sum(2 * count * OCC for _, count in groups)
         r, c = iota((NBF, width), 0), iota((NBF, width), 1)
         c32, r32 = iota((32, width), 1), iota((32, width), 0)
         pick, qp, at = r < 0, c32 < 0, 0
         for first, count in groups:
             half = count * OCC
-            pick |= (r == col * ROWS_P + first + (c - at) % half // OCC) & (c >= at) & (c < at + 2 * half)
+            pick |= (r == dev * ROWS_P + first + (c - at) % half // OCC) & (c >= at) & (c < at + 2 * half)
             qp |= (r32 // OCC % 2 == (c32 - at) // half) & (c32 >= at) & (c32 < at + 2 * half)
             at += 2 * half
         placed = dot(co_i, one_hot(pick))
         return jnp.where(qp & (r32 // 8 == c32 % OCC), placed, 0.0).astype(BF16)
 
-    w2[...] = spread([(0, ROWS_P)])
-    w2a[...] = spread([(0, 16)])
-    w2b[...] = spread([(16, 8), (24, 8)])
+    w2[0] = spread(col, [(0, ROWS_P)])
+    w2[1] = spread(other, [(0, ROWS_P)])
+    w2a[...] = spread(col, [(0, 16)])
+    w2b[...] = spread(col, [(16, 8), (24, 8)])
 
     b, c = iota((VIRT, 256), 0), iota((VIRT, 256), 1)
     halves = dot_tn(cv, one_hot((b == (c // NBF) * HALF + c % 64) & (c % 64 < HALF)))
@@ -138,8 +154,6 @@
     for i in range(OCC):
         cvd[:, i * NBF:(i + 1) * NBF] = jnp.where(r % OCC == i, rows, 0.0).astype(BF16)
 
-    pl.semaphore_wait(barrier, DEVS - 1)
-
     def contract_r(slot, blocks):
         left = lhs1[...]
         for qp, pb, at in blocks:
@@ -173,44 +187,67 @@
     upper = [b for b in whole if b[1] < 16]
     lower = [b for b in whole if b[1] >= 16]
 
-    def refill(step, slot):
-        @pl.when(step + SLOTS < LOOPED)
+    def refill(tile):
+        @pl.when(tile + SLOTS < LOOPED)
         def _():
-            fetch(step + SLOTS, slot).start(priority=1)
-
-        for n in range(len(PIECES)):
-            @pl.when(step + SLOTS == PIECES[n][0])
+            fetch(tile + SLOTS, slot_of(tile)).start(priority=1)
+
+        for step in range(LOOPED, STEPS):
+            @pl.when(tile + SLOTS == step)
             def _():
-                fetch_piece(n).start(priority=1)
-
-    def beside(step, slot, mine):
+                for n in range(len(PIECES)):
+                    if PIECES[n][0] == step:
+                        fetch_piece(n).start(priority=1)
+
+    def beside(slot, mine, before, weights):
         half = contract_s(t1[...])
         contract_r(slot, mine[:4])
-        e_part = dot(w2[...], half)
+        e_part = dot(weights, half)
         contract_r(slot, mine[4:])
-        pack(step - 1, e_part)
-        send(step - 1, 0)
-
-    def step_body(step, carry):
-        slot = lax.rem(step, SLOTS)
-        fetch(step, slot).wait()
-        beside(step, slot, whole)
-        refill(step, slot)
+        pack(before, e_part)
+        send(before, 0)
+
+    def taken(n):
+        return (n - 1) // EVERY
+
+    def own(n):
+        return GIVEN + n - taken(n)
+
+    def step_body(n, carry):
+        theirs, before_theirs = lax.rem(n, EVERY) == 0, (lax.rem(n, EVERY) == 1) & (n > 1)
+        slot = jnp.where(theirs, SLOTS + taken(n), slot_of(own(n)))
+        before = jnp.where(before_theirs, taken(n) - 1, own(n) - 1)
+
+        for k in range(GIVEN):
+            @pl.when(n == (k + 1) * EVERY)
+            def _():
+                gifts[k].wait_recv()
+
+        @pl.when(jnp.logical_not(theirs))
+        def _():
+            fetch(own(n), slot_of(own(n))).wait()
+
+        beside(slot, whole, before, w2[jnp.where(before_theirs, 1, 0)])
+
+        @pl.when(jnp.logical_not(theirs))
+        def _():
+            refill(own(n))
+
         return carry
 
-    fetch(0, 0).wait()
+    fetch(GIVEN, 0).wait()
     contract_r(0, whole)
-    refill(0, 0)
+    refill(GIVEN)
     lax.fori_loop(1, LOOPED, step_body, 0)
 
-    slot = LOOPED % SLOTS
+    slot = (LOOPED - GIVEN) % SLOTS
     fetch_piece(0).wait()
-    beside(LOOPED, slot, upper)
+    beside(slot, upper, LOOPED - 1, w2[0])
     fetch_piece(1).wait()
     contract_r(slot, lower)
-    slot = LAST % SLOTS
+    slot = (LAST - GIVEN) % SLOTS
     fetch_piece(2).wait()
-    beside(LAST, slot, [b for b in blocks(0, 16, 0) if b[1] < 8])
+    beside(slot, [b for b in blocks(0, 16, 0) if b[1] < 8], LOOPED, w2[0])
     fetch_piece(3).wait()
     contract_r(slot, [b for b in blocks(0, 16, 0) if b[1] >= 8])
     fetch_piece(4).wait()
@@ -242,6 +279,8 @@
     arrived(recv.at[LAST, pl.ds(0, DEVS - 1)], 1)
     sent = sendbuf.at[:, pl.ds(0, DEVS - 1)]
     pltpu.make_async_copy(sent, sent, send_sem).wait()
+    for gift in gifts:
+        gift.wait_send()
 
 
 def finish(recv, base, cvd, out_ref):
@@ -270,12 +309,12 @@
             in_specs=[hbm] * 3,
             out_specs=[vmem] * 3,
             scratch_shapes=[
-                pltpu.VMEM((SLOTS, ROWS_P, TILE_Q, NBF, NBF), BF16),
+                pltpu.VMEM((SLOTS + GIVEN, ROWS_P, TILE_Q, NBF, NBF), BF16),
                 pltpu.VMEM((OCC, NBF), BF16),
                 pltpu.VMEM((VIRT, NBF), BF16),
                 pltpu.VMEM((16, 256), BF16),
                 pltpu.VMEM((256, 256), BF16),
-                pltpu.VMEM((32, 256), BF16),
+                pltpu.VMEM((2, 32, 256), BF16),
                 pltpu.VMEM((32, NBF), BF16),
                 pltpu.VMEM((32, NBF), BF16),
                 pltpu.VMEM((512, 512), BF16),
@@ -283,6 +322,8 @@
                 pltpu.VMEM((STEPS, DEVS, 8, NBF), F32),
                 pltpu.SemaphoreType.DMA,
                 pltpu.SemaphoreType.DMA((2,)),
+                pltpu.SemaphoreType.DMA((GIVEN,)),
+                pltpu.SemaphoreType.DMA((GIVEN,)),
             ],
             compiler_params=pltpu.CompilerParams(
                 collective_id=0, has_side_effects=True, vmem_limit_bytes=48 * 1024 * 1024),

time: 28 us -> 25.9 us (0.925)
  Pallas kernels: 27.9 us -> 25.8 us
    pallas_call x1, Pallas kernels: 27 us -> 24.9 us  [local_block(): pl.pallas_call(kernel, out_shape=[jax.ShapeDtypeStruct((STEPS, DEVS, 8, N...]
where the time goes in v5:
time: 25.9 us; the launch traced here: 25.8 us
  Pallas kernels  25.8 us (100%)
    pallas_call x1, Pallas kernels, local_block(): pl.pallas_call(kernel, out_shape=[jax.ShapeDtypeStruct((STEPS, DEVS, 8, N...  24.9 us
    pallas_call x1, Pallas kernels, local_block(): pl.pallas_call(finish, out_shape=jax.ShapeDtypeStruct((OCC, HALF, VIRT),...  0.88 us

profile of v5, /device:TPU:0, one launch (start us, length us, event | category | flops | bytes accessed | tf_op | source)
XLA Modules:
  0.0 25.8 jit_solution(870265883861611157)
XLA Ops:
  0.0 24.9 %shard_map.37 = (f32[16,8,8,128]{3,2,1,0:T(8,128)S(1)}, f32[64,512]{1,0:T(8,128)S(1)}, bf16[256,512]{1,0:T(8,128)(2,1)S(1)}) custom-call(bf16[32,64,128,128]{3,2,1,0:T(8,128)(2,1)} %refs_0_.1, bf16[4,128]{1,0:T(4,128)(2,1)} %bitcast.4, bf16[112,128]{1,0:T(8,128)(2,1)} %bitcast.3), custom_call_target="tpu_custom_call" | custom-call | tf_op jit(solution)/shard_map/pallas_call | solution.py:302
  24.9 0.9 %shard_map.38 = f32[4,56,112]{2,1,0:T(8,128)} custom-call(f32[16,8,8,128]{3,2,1,0:T(8,128)S(1)} %get-tuple-element.8.recv, f32[64,512]{1,0:T(8,128)S(1)} %get-tuple-element.9.base, bf16[256,512]{1,0:T(8,128)(2,1)S(1)} %get-tuple-element.10.cvd), custom_call_target="tpu_custom_call" | custom-call | tf_op jit(solution)/shard_map/pallas_call | solution.py:332

commit v6 on v5

--- a/solution.py
+++ b/solution.py
@@ -21,7 +21,7 @@
 STEPS = ROWS_Q // TILE_Q
 SLOTS = 6
 GIVEN = 2
-EVERY = 6
+TURNS = (5, 11)
 DEVS = 8
 COLS = 4
 PIECES = ((14, 0, 16), (14, 16, 16), (15, 0, 8), (15, 8, 8), (15, 16, 8), (15, 24, 8))
@@ -65,7 +65,7 @@
     )
 
 
-def body(a_hbm, co_hbm, cv_hbm, recv, base, cvd, abuf, co_ref, cv_ref, lhs1, cv2, w2, w2a, w2b, cvx, t1, sendbuf,
+def body(a_hbm, co_hbm, cv_hbm, recv, base, cvd, abuf, co_ref, cv_ref, lhs1, cv2, w2, w2a, w2b, w2x, cvx, t1, t1x, sendbuf,
          send_sem, recv_sem, give_sem, take_sem, a_sem, l_sem, c_sem):
     row, col = lax.axis_index("dev2"), lax.axis_index("dev")
     me = row * COLS + col
@@ -100,13 +100,20 @@
     pl.semaphore_wait(barrier, DEVS - 1)
 
     other = 2 * x + 1 - core
+    given = [(0, ROWS_P, k) for k in range(GIVEN)] + [(16, 16, LOOPED)]
     gifts = []
-    for k in range(GIVEN):
+    for k, (first, count, tile) in enumerate(given):
         gifts.append(pltpu.make_async_remote_copy(
-            src_ref=a_hbm.at[:, pl.ds(k * TILE_Q, TILE_Q)], dst_ref=abuf.at[SLOTS + k],
+            src_ref=a_hbm.at[pl.ds(first, count), pl.ds(tile * TILE_Q, TILE_Q)],
+            dst_ref=abuf.at[SLOTS + k, pl.ds(first, count)],
             send_sem=give_sem.at[k], recv_sem=take_sem.at[k],
             device_id={"dev2": row, "dev": other}, device_id_type=MESH))
+    for k in range(GIVEN):
         gifts[k].start()
+
+    @pl.when(core == 0)
+    def _():
+        gifts[GIVEN].start()
 
     co_copy.wait()
     cv_copy.wait()
@@ -136,6 +143,7 @@
     w2[1] = spread(other, [(0, ROWS_P)])
     w2a[...] = spread(col, [(0, 16)])
     w2b[...] = spread(col, [(16, 8), (24, 8)])
+    w2x[...] = spread(other, [(16, 16)])
 
     b, c = iota((VIRT, 256), 0), iota((VIRT, 256), 1)
     halves = dot_tn(cv, one_hot((b == (c // NBF) * HALF + c % 64) & (c % 64 < HALF)))
@@ -154,7 +162,7 @@
     for i in range(OCC):
         cvd[:, i * NBF:(i + 1) * NBF] = jnp.where(r % OCC == i, rows, 0.0).astype(BF16)
 
-    def contract_r(slot, blocks):
+    def contract_r(slot, blocks, ref=t1):
         left = lhs1[...]
         for qp, pb, at in blocks:
             parts = []
@@ -162,10 +170,14 @@
                 rhs = jnp.concatenate(
                     [abuf[slot, p0:p0 + 2, 2 * qp + par].reshape(256, NBF) for par in range(2)], axis=1)
                 parts.append(dot(left, rhs)[:8])
-            t1[at:at + 16, :] = jnp.concatenate(parts, axis=0).astype(BF16)
+            ref[at:at + 16, :] = jnp.concatenate(parts, axis=0).astype(BF16)
 
     def contract_s(t_one):
-        return dot(t_one, cv2[...]).astype(BF16)
+        rows = t_one.shape[0]
+        if rows < NBF:
+            return dot(t_one, cv2[...]).astype(BF16)
+        parts = [dot(t_one[k:k + rows // 2], cv2[...]).astype(BF16) for k in (0, rows // 2)]
+        return jnp.concatenate(parts, axis=0)
 
     def pack(step, e_part):
         for j in range(OCC):
@@ -196,30 +208,39 @@
             @pl.when(tile + SLOTS == step)
             def _():
                 for n in range(len(PIECES)):
-                    if PIECES[n][0] == step:
+                    if PIECES[n][0] == step and n != 1:
                         fetch_piece(n).start(priority=1)
 
-    def beside(slot, mine, before, weights):
+        @pl.when((tile + SLOTS == LOOPED) & (core == 1))
+        def _():
+            fetch_piece(1).start(priority=1)
+
+    def beside(slot, mine, before, weights, more=False):
         half = contract_s(t1[...])
+        if more:
+            extra = contract_s(t1x[...])
         contract_r(slot, mine[:4])
         e_part = dot(weights, half)
+        if more:
+            e_part += dot(w2x[...], extra)
         contract_r(slot, mine[4:])
         pack(before, e_part)
         send(before, 0)
 
     def taken(n):
-        return (n - 1) // EVERY
+        return sum(jnp.where(n > turn, 1, 0) for turn in TURNS)
 
     def own(n):
         return GIVEN + n - taken(n)
 
     def step_body(n, carry):
-        theirs, before_theirs = lax.rem(n, EVERY) == 0, (lax.rem(n, EVERY) == 1) & (n > 1)
+        theirs = (n == TURNS[0]) | (n == TURNS[1])
+        before_theirs = (n == TURNS[0] + 1) | (n == TURNS[1] + 1)
         slot = jnp.where(theirs, SLOTS + taken(n), slot_of(own(n)))
         before = jnp.where(before_theirs, taken(n) - 1, own(n) - 1)
 
         for k in range(GIVEN):
-            @pl.when(n == (k + 1) * EVERY)
+            @pl.when(n == TURNS[k])
             def _():
                 gifts[k].wait_recv()
 
@@ -243,11 +264,26 @@
     slot = (LOOPED - GIVEN) % SLOTS
     fetch_piece(0).wait()
     beside(slot, upper, LOOPED - 1, w2[0])
-    fetch_piece(1).wait()
-    contract_r(slot, lower)
-    slot = (LAST - GIVEN) % SLOTS
-    fetch_piece(2).wait()
-    beside(slot, [b for b in blocks(0, 16, 0) if b[1] < 8], LOOPED, w2[0])
+    first = [b for b in blocks(0, 16, 0) if b[1] < 8]
+    last_slot = (LAST - GIVEN) % SLOTS
+
+    @pl.when(core == 0)
+    def _():
+        for qp in range(2):
+            t1[qp * 128 + 64:(qp + 1) * 128, :] = jnp.zeros((64, 256), BF16)
+        fetch_piece(2).wait()
+        beside(last_slot, first, LOOPED, w2[0])
+
+    @pl.when(core == 1)
+    def _():
+        fetch_piece(1).wait()
+        contract_r(slot, lower)
+        gifts[GIVEN].wait_recv()
+        contract_r(SLOTS + GIVEN, blocks(16, 16, 0), t1x)
+        fetch_piece(2).wait()
+        beside(last_slot, first, LOOPED, w2[0], more=True)
+
+    slot = last_slot
     fetch_piece(3).wait()
     contract_r(slot, [b for b in blocks(0, 16, 0) if b[1] >= 8])
     fetch_piece(4).wait()
@@ -279,8 +315,12 @@
     arrived(recv.at[LAST, pl.ds(0, DEVS - 1)], 1)
     sent = sendbuf.at[:, pl.ds(0, DEVS - 1)]
     pltpu.make_async_copy(sent, sent, send_sem).wait()
-    for gift in gifts:
-        gift.wait_send()
+    for k in range(GIVEN):
+        gifts[k].wait_send()
+
+    @pl.when(core == 0)
+    def _():
+        gifts[GIVEN].wait_send()
 
 
 def finish(recv, base, cvd, out_ref):
@@ -309,7 +349,7 @@
             in_specs=[hbm] * 3,
             out_specs=[vmem] * 3,
             scratch_shapes=[
-                pltpu.VMEM((SLOTS + GIVEN, ROWS_P, TILE_Q, NBF, NBF), BF16),
+                pltpu.VMEM((SLOTS + GIVEN + 1, ROWS_P, TILE_Q, NBF, NBF), BF16),
                 pltpu.VMEM((OCC, NBF), BF16),
                 pltpu.VMEM((VIRT, NBF), BF16),
                 pltpu.VMEM((16, 256), BF16),
@@ -317,13 +357,15 @@
                 pltpu.VMEM((2, 32, 256), BF16),
                 pltpu.VMEM((32, NBF), BF16),
                 pltpu.VMEM((32, NBF), BF16),
+                pltpu.VMEM((32, NBF), BF16),
                 pltpu.VMEM((512, 512), BF16),
                 pltpu.VMEM((256, 256), BF16),
+                pltpu.VMEM((NBF, 256), BF16),
                 pltpu.VMEM((STEPS, DEVS, 8, NBF), F32),
                 pltpu.SemaphoreType.DMA,
                 pltpu.SemaphoreType.DMA((2,)),
-                pltpu.SemaphoreType.DMA((GIVEN,)),
-                pltpu.SemaphoreType.DMA((GIVEN,)),
+                pltpu.SemaphoreType.DMA((GIVEN + 1,)),
+                pltpu.SemaphoreType.DMA((GIVEN + 1,)),
             ],
             compiler_params=pltpu.CompilerParams(
                 collective_id=0, has_side_effects=True, vmem_limit_bytes=48 * 1024 * 1024),

time: 25.9 us -> 25.3 us (0.977)
  Pallas kernels: 25.8 us -> 25.2 us
    pallas_call x1, Pallas kernels: 24.9 us -> 24.3 us  [local_block(): pl.pallas_call(kernel, out_shape=[jax.ShapeDtypeStruct((STEPS, DEVS, 8, N...]
where the time goes in v6:
time: 25.3 us; the launch traced here: 25.2 us
  Pallas kernels  25.2 us (100%)
    pallas_call x1, Pallas kernels, local_block(): pl.pallas_call(kernel, out_shape=[jax.ShapeDtypeStruct((STEPS, DEVS, 8, N...  24.3 us
    pallas_call x1, Pallas kernels, local_block(): pl.pallas_call(finish, out_shape=jax.ShapeDtypeStruct((OCC, HALF, VIRT),...  0.88 us

profile of v6, /device:TPU:0, one launch (start us, length us, event | category | flops | bytes accessed | tf_op | source)
XLA Modules:
  0.0 25.2 jit_solution(6411219041887185368)
XLA Ops:
  0.0 24.3 %shard_map.37 = (f32[16,8,8,128]{3,2,1,0:T(8,128)S(1)}, f32[64,512]{1,0:T(8,128)S(1)}, bf16[256,512]{1,0:T(8,128)(2,1)S(1)}) custom-call(bf16[32,64,128,128]{3,2,1,0:T(8,128)(2,1)} %refs_0_.1, bf16[4,128]{1,0:T(4,128)(2,1)} %bitcast.4, bf16[112,128]{1,0:T(8,128)(2,1)} %bitcast.3), custom_call_target="tpu_custom_call" | custom-call | tf_op jit(solution)/shard_map/pallas_call | solution.py:342
  24.3 0.9 %shard_map.38 = f32[4,56,112]{2,1,0:T(8,128)} custom-call(f32[16,8,8,128]{3,2,1,0:T(8,128)S(1)} %get-tuple-element.8.recv, f32[64,512]{1,0:T(8,128)S(1)} %get-tuple-element.9.base, bf16[256,512]{1,0:T(8,128)(2,1)S(1)} %get-tuple-element.10.cvd), custom_call_target="tpu_custom_call" | custom-call | tf_op jit(solution)/shard_map/pallas_call | solution.py:374

commit v7 on v6

--- a/solution.py
+++ b/solution.py
@@ -19,14 +19,16 @@
 HALF = VIRT // 2
 TILE_Q = 4
 STEPS = ROWS_Q // TILE_Q
-SLOTS = 6
-GIVEN = 2
-TURNS = (5, 11)
+SLOTS = 5
+OWN = 24
+GIFT = ROWS_P - OWN
 DEVS = 8
 COLS = 4
-PIECES = ((14, 0, 16), (14, 16, 16), (15, 0, 8), (15, 8, 8), (15, 16, 8), (15, 24, 8))
+PIECES = ((13, 0, 16), (13, 16, 16), (14, 0, 8), (14, 8, 8), (14, 16, 16), (15, 0, 8), (15, 8, 8), (15, 16, 8), (15, 24, 8))
+SHARED = 14
 LAST = STEPS - 1
-LOOPED = STEPS - 2
+LOOPED = STEPS - 3
+GIVEN = 8
 
 
 def iota(shape, dim):
@@ -60,37 +62,49 @@
     pl.run_scoped(
         functools.partial(body, *refs),
         pltpu.SemaphoreType.DMA((SLOTS,)),
+        pltpu.SemaphoreType.DMA((LOOPED,)),
         pltpu.SemaphoreType.DMA((len(PIECES),)),
         pltpu.SemaphoreType.DMA((2,)),
+        pltpu.SemaphoreType.DMA,
+        pltpu.SemaphoreType.DMA((2,)),
+        pltpu.SemaphoreType.DMA((2,)),
+        pltpu.SemaphoreType.DMA((GIVEN + 1,)),
     )
 
 
-def body(a_hbm, co_hbm, cv_hbm, recv, base, cvd, abuf, co_ref, cv_ref, lhs1, cv2, w2, w2a, w2b, w2x, cvx, t1, t1x, sendbuf,
-         send_sem, recv_sem, give_sem, take_sem, a_sem, l_sem, c_sem):
+def body(a_hbm, co_hbm, cv_hbm, recv, base, cvd, abuf, land, ends, xbuf, co_ref, cv_ref, lhs1, cv2, w2, w2a, w2b, w2x, cvx, t1, t1x, sendbuf,
+         a_sem, land_sem, l_sem, c_sem, send_sem, recv_sem, give_sem, take_sem):
     row, col = lax.axis_index("dev2"), lax.axis_index("dev")
     me = row * COLS + col
 
-    def slot_of(tile):
-        return lax.rem(tile - GIVEN, SLOTS)
-
-    def fetch(tile, slot):
-        return pltpu.make_async_copy(a_hbm.at[:, pl.ds(tile * TILE_Q, TILE_Q)], abuf.at[slot], a_sem.at[slot])
+    def fetch(tile):
+        slot = lax.rem(tile, SLOTS)
+        return pltpu.make_async_copy(
+            a_hbm.at[pl.ds(0, OWN), pl.ds(tile * TILE_Q, TILE_Q)], abuf.at[slot], a_sem.at[slot])
+
+    def fetch_rest(tile):
+        return pltpu.make_async_copy(
+            a_hbm.at[pl.ds(OWN, GIFT), pl.ds(tile * TILE_Q, TILE_Q)], land.at[tile], land_sem.at[tile])
 
     def fetch_piece(n):
         tile, first, count = PIECES[n]
         part = pl.ds(first, count)
         return pltpu.make_async_copy(
-            a_hbm.at[part, pl.ds(tile * TILE_Q, TILE_Q)], abuf.at[(tile - GIVEN) % SLOTS, part], l_sem.at[n])
+            a_hbm.at[part, pl.ds(tile * TILE_Q, TILE_Q)], ends.at[tile - LOOPED, part], l_sem.at[n])
 
     co_copy = pltpu.make_async_copy(co_hbm, co_ref, c_sem.at[0])
     cv_copy = pltpu.make_async_copy(cv_hbm, cv_ref, c_sem.at[1])
     co_copy.start()
     cv_copy.start()
-    for s in range(SLOTS):
-        fetch(GIVEN + s, s).start(priority=1)
+    for tile in range(SLOTS):
+        fetch(tile).start(priority=1)
+        if tile % 3 == 0:
+            fetch_rest(tile).start(priority=1)
 
     x, core = col // 2, lax.rem(col, 2)
     far_row, far_x = 1 - row, 1 - x
+    giver, taker = (row + x == 2) & (core == 0), (row + x == 2) & (core == 1)
+    plain = row + x < 2
     peers = [(far_row, 2 * far_x), (far_row, 2 * far_x + 1), (far_row, 2 * x), (far_row, 2 * x + 1),
              (row, 2 * far_x), (row, 2 * far_x + 1), (row, 2 * x + 1 - core)]
 
@@ -100,18 +114,18 @@
     pl.semaphore_wait(barrier, DEVS - 1)
 
     other = 2 * x + 1 - core
-    given = [(0, ROWS_P, k) for k in range(GIVEN)] + [(16, 16, LOOPED)]
     gifts = []
-    for k, (first, count, tile) in enumerate(given):
+    for tile in [t for t in range(LOOPED) if t % 3] + [SHARED]:
+        late = tile == SHARED
         gifts.append(pltpu.make_async_remote_copy(
-            src_ref=a_hbm.at[pl.ds(first, count), pl.ds(tile * TILE_Q, TILE_Q)],
-            dst_ref=abuf.at[SLOTS + k, pl.ds(first, count)],
-            send_sem=give_sem.at[k], recv_sem=take_sem.at[k],
+            src_ref=a_hbm.at[pl.ds(16, 16) if late else pl.ds(OWN, GIFT), pl.ds(tile * TILE_Q, TILE_Q)],
+            dst_ref=xbuf if late else land.at[tile],
+            send_sem=give_sem.at[1 if late else 0], recv_sem=take_sem.at[len(gifts)],
             device_id={"dev2": row, "dev": other}, device_id_type=MESH))
     for k in range(GIVEN):
         gifts[k].start()
 
-    @pl.when(core == 0)
+    @pl.when(giver)
     def _():
         gifts[GIVEN].start()
 
@@ -139,8 +153,14 @@
         placed = dot(co_i, one_hot(pick))
         return jnp.where(qp & (r32 // 8 == c32 % OCC), placed, 0.0).astype(BF16)
 
-    w2[0] = spread(col, [(0, ROWS_P)])
-    w2[1] = spread(other, [(0, ROWS_P)])
+    r, c = iota((NBF, 256), 0), iota((NBF, 256), 1)
+    p = c % NBF // OCC
+    for k in range(2):
+        source = jnp.where((p < OWN) | (k == 0), col, other)
+        placed = dot(co_i, one_hot(r == source * ROWS_P + p))
+        c32, r32 = iota((32, 256), 1), iota((32, 256), 0)
+        keep = (r32 // OCC % 2 == c32 // NBF) & (r32 // 8 == c32 % OCC)
+        w2[k] = jnp.where(keep, placed, 0.0).astype(BF16)
     w2a[...] = spread(col, [(0, 16)])
     w2b[...] = spread(col, [(16, 8), (24, 8)])
     w2x[...] = spread(other, [(16, 16)])
@@ -162,15 +182,20 @@
     for i in range(OCC):
         cvd[:, i * NBF:(i + 1) * NBF] = jnp.where(r % OCC == i, rows, 0.0).astype(BF16)
 
-    def contract_r(slot, blocks, ref=t1):
+    def contract_r(rows_of, blocks, ref=t1):
         left = lhs1[...]
         for qp, pb, at in blocks:
             parts = []
             for p0 in (pb, pb + 2):
-                rhs = jnp.concatenate(
-                    [abuf[slot, p0:p0 + 2, 2 * qp + par].reshape(256, NBF) for par in range(2)], axis=1)
+                rhs = jnp.concatenate([rows_of(p0, 2 * qp + par).reshape(256, NBF) for par in range(2)], axis=1)
                 parts.append(dot(left, rhs)[:8])
             ref[at:at + 16, :] = jnp.concatenate(parts, axis=0).astype(BF16)
+
+    def looped(tile, slot):
+        return lambda p0, q: abuf[slot, p0:p0 + 2, q] if p0 < OWN else land[tile, p0 - OWN:p0 - OWN + 2, q]
+
+    def ending(tile):
+        return lambda p0, q: ends[tile - LOOPED, p0:p0 + 2, q]
 
     def contract_s(t_one):
         rows = t_one.shape[0]
@@ -200,98 +225,113 @@
     lower = [b for b in whole if b[1] >= 16]
 
     def refill(tile):
-        @pl.when(tile + SLOTS < LOOPED)
+        new = tile + SLOTS
+
+        @pl.when(new < LOOPED)
         def _():
-            fetch(tile + SLOTS, slot_of(tile)).start(priority=1)
+            fetch(new).start(priority=1)
+
+        @pl.when((new < LOOPED) & (lax.rem(new, 3) == 0))
+        def _():
+            fetch_rest(new).start(priority=1)
 
         for step in range(LOOPED, STEPS):
-            @pl.when(tile + SLOTS == step)
+            @pl.when(new == step)
             def _():
                 for n in range(len(PIECES)):
-                    if PIECES[n][0] == step and n != 1:
+                    if PIECES[n][0] == step and PIECES[n] != (SHARED, 16, 16):
                         fetch_piece(n).start(priority=1)
 
-        @pl.when((tile + SLOTS == LOOPED) & (core == 1))
+        @pl.when((new == SHARED) & jnp.logical_not(giver))
         def _():
-            fetch_piece(1).start(priority=1)
-
-    def beside(slot, mine, before, weights, more=False):
+            fetch_piece(4).start(priority=1)
+
+    def beside(rows_of, mine, before, weights, more=False):
         half = contract_s(t1[...])
         if more:
             extra = contract_s(t1x[...])
-        contract_r(slot, mine[:4])
+        contract_r(rows_of, mine[:4])
         e_part = dot(weights, half)
         if more:
             e_part += dot(w2x[...], extra)
-        contract_r(slot, mine[4:])
+        contract_r(rows_of, mine[4:])
         pack(before, e_part)
         send(before, 0)
 
-    def taken(n):
-        return sum(jnp.where(n > turn, 1, 0) for turn in TURNS)
-
-    def own(n):
-        return GIVEN + n - taken(n)
-
-    def step_body(n, carry):
-        theirs = (n == TURNS[0]) | (n == TURNS[1])
-        before_theirs = (n == TURNS[0] + 1) | (n == TURNS[1] + 1)
-        slot = jnp.where(theirs, SLOTS + taken(n), slot_of(own(n)))
-        before = jnp.where(before_theirs, taken(n) - 1, own(n) - 1)
-
-        for k in range(GIVEN):
-            @pl.when(n == TURNS[k])
-            def _():
-                gifts[k].wait_recv()
-
-        @pl.when(jnp.logical_not(theirs))
+    def step_body(tile, carry):
+        fetch(tile).wait()
+
+        @pl.when(lax.rem(tile, 3) == 0)
         def _():
-            fetch(own(n), slot_of(own(n))).wait()
-
-        beside(slot, whole, before, w2[jnp.where(before_theirs, 1, 0)])
-
-        @pl.when(jnp.logical_not(theirs))
+            fetch_rest(tile).wait()
+
+        @pl.when(lax.rem(tile, 3) != 0)
         def _():
-            refill(own(n))
-
+            view = land.at[tile]
+            pltpu.make_async_copy(view, view, take_sem.at[tile - tile // 3 - 1]).wait()
+
+        mixed = jnp.where(lax.rem(tile - 1, 3) == 0, 0, 1)
+        beside(looped(tile, lax.rem(tile, SLOTS)), whole, tile - 1, w2[mixed])
+        refill(tile)
         return carry
 
-    fetch(GIVEN, 0).wait()
-    contract_r(0, whole)
-    refill(GIVEN)
+    fetch(0).wait()
+    fetch_rest(0).wait()
+    contract_r(looped(0, 0), whole)
+    refill(0)
     lax.fori_loop(1, LOOPED, step_body, 0)
 
-    slot = (LOOPED - GIVEN) % SLOTS
     fetch_piece(0).wait()
-    beside(slot, upper, LOOPED - 1, w2[0])
+    beside(ending(LOOPED), upper, LOOPED - 1, w2[0])
+    fetch_piece(1).wait()
+    contract_r(ending(LOOPED), lower)
     first = [b for b in blocks(0, 16, 0) if b[1] < 8]
-    last_slot = (LAST - GIVEN) % SLOTS
-
-    @pl.when(core == 0)
+    second = [b for b in blocks(0, 16, 0) if b[1] >= 8]
+
+    @pl.when(giver)
     def _():
-        for qp in range(2):
-            t1[qp * 128 + 64:(qp + 1) * 128, :] = jnp.zeros((64, 256), BF16)
         fetch_piece(2).wait()
-        beside(last_slot, first, LOOPED, w2[0])
-
-    @pl.when(core == 1)
+        beside(ending(SHARED), first, SHARED - 1, w2[0])
+        fetch_piece(3).wait()
+        contract_r(ending(SHARED), second)
+        fetch_piece(5).wait()
+        half = contract_s(t1[:128, :])
+        contract_r(ending(LAST), first)
+        pack(SHARED, dot(w2a[...], half))
+        send(SHARED, 0)
+        fetch_piece(6).wait()
+        contract_r(ending(LAST), second)
+
+    @pl.when(plain)
     def _():
-        fetch_piece(1).wait()
-        contract_r(slot, lower)
+        fetch_piece(2).wait()
+        fetch_piece(3).wait()
+        beside(ending(SHARED), upper, SHARED - 1, w2[0])
+        fetch_piece(4).wait()
+        contract_r(ending(SHARED), lower)
+        fetch_piece(5).wait()
+        fetch_piece(6).wait()
+        beside(ending(LAST), first + second, SHARED, w2[0])
+
+    @pl.when(taker)
+    def _():
+        fetch_piece(2).wait()
+        fetch_piece(3).wait()
+        beside(ending(SHARED), upper, SHARED - 1, w2[0])
         gifts[GIVEN].wait_recv()
-        contract_r(SLOTS + GIVEN, blocks(16, 16, 0), t1x)
-        fetch_piece(2).wait()
-        beside(last_slot, first, LOOPED, w2[0], more=True)
-
-    slot = last_slot
-    fetch_piece(3).wait()
-    contract_r(slot, [b for b in blocks(0, 16, 0) if b[1] >= 8])
-    fetch_piece(4).wait()
+        fetch_piece(4).wait()
+        contract_r(ending(SHARED), lower)
+        contract_r(lambda p0, q: xbuf[p0 - 16:p0 - 14, q], blocks(16, 16, 0), t1x)
+        fetch_piece(5).wait()
+        fetch_piece(6).wait()
+        beside(ending(LAST), first + second, SHARED, w2[0], more=True)
+
+    fetch_piece(7).wait()
     half = contract_s(t1[:128, :])
-    contract_r(slot, blocks(16, 8, 128))
+    contract_r(ending(LAST), blocks(16, 8, 128))
     e_part = dot(w2a[...], half)
-    fetch_piece(5).wait()
-    contract_r(slot, blocks(24, 8, 192))
+    fetch_piece(8).wait()
+    contract_r(ending(LAST), blocks(24, 8, 192))
     half = jnp.concatenate([contract_s(t1[128:192, :]), contract_s(t1[192:, :])], axis=0)
     e_part += dot(w2b[...], half)
     pack(LAST, e_part)
@@ -315,10 +355,10 @@
     arrived(recv.at[LAST, pl.ds(0, DEVS - 1)], 1)
     sent = sendbuf.at[:, pl.ds(0, DEVS - 1)]
     pltpu.make_async_copy(sent, sent, send_sem).wait()
-    for k in range(GIVEN):
-        gifts[k].wait_send()
-
-    @pl.when(core == 0)
+    view = land.at[pl.ds(0, GIVEN)]
+    pltpu.make_async_copy(view, view, give_sem.at[0]).wait()
+
+    @pl.when(giver)
     def _():
         gifts[GIVEN].wait_send()
 
@@ -349,7 +389,10 @@
             in_specs=[hbm] * 3,
             out_specs=[vmem] * 3,
             scratch_shapes=[
-                pltpu.VMEM((SLOTS + GIVEN + 1, ROWS_P, TILE_Q, NBF, NBF), BF16),
+                pltpu.VMEM((SLOTS, OWN, TILE_Q, NBF, NBF), BF16),
+                pltpu.VMEM((LOOPED, GIFT, TILE_Q, NBF, NBF), BF16),
+                pltpu.VMEM((STEPS - LOOPED, ROWS_P, TILE_Q, NBF, NBF), BF16),
+                pltpu.VMEM((16, TILE_Q, NBF, NBF), BF16),
                 pltpu.VMEM((OCC, NBF), BF16),
                 pltpu.VMEM((VIRT, NBF), BF16),
                 pltpu.VMEM((16, 256), BF16),
@@ -362,10 +405,6 @@
                 pltpu.VMEM((256, 256), BF16),
                 pltpu.VMEM((NBF, 256), BF16),
                 pltpu.VMEM((STEPS, DEVS, 8, NBF), F32),
-                pltpu.SemaphoreType.DMA,
-                pltpu.SemaphoreType.DMA((2,)),
-                pltpu.SemaphoreType.DMA((GIVEN + 1,)),
-                pltpu.SemaphoreType.DMA((GIVEN + 1,)),
             ],
             compiler_params=pltpu.CompilerParams(
                 collective_id=0, has_side_effects=True, vmem_limit_bytes=48 * 1024 * 1024),

time: 25.3 us -> 24.9 us (0.984)
  Pallas kernels: 25.2 us -> 24.8 us
    pallas_call x1, Pallas kernels: 24.3 us -> 23.9 us  [local_block(): pl.pallas_call(kernel, out_shape=[jax.ShapeDtypeStruct((STEPS, DEVS, 8, N...]
where the time goes in v7:
time: 24.9 us; the launch traced here: 24.8 us
  Pallas kernels  24.8 us (100%)
    pallas_call x1, Pallas kernels, local_block(): pl.pallas_call(kernel, out_shape=[jax.ShapeDtypeStruct((STEPS, DEVS, 8, N...  23.9 us
    pallas_call x1, Pallas kernels, local_block(): pl.pallas_call(finish, out_shape=jax.ShapeDtypeStruct((OCC, HALF, VIRT),...  0.88 us

profile of v7, /device:TPU:0, one launch (start us, length us, event | category | flops | bytes accessed | tf_op | source)
XLA Modules:
  0.0 24.8 jit_solution(16564335331424127515)
XLA Ops:
  0.0 23.9 %shard_map.37 = (f32[16,8,8,128]{3,2,1,0:T(8,128)S(1)}, f32[64,512]{1,0:T(8,128)S(1)}, bf16[256,512]{1,0:T(8,128)(2,1)S(1)}) custom-call(bf16[32,64,128,128]{3,2,1,0:T(8,128)(2,1)} %refs_0_.1, bf16[4,128]{1,0:T(4,128)(2,1)} %bitcast.4, bf16[112,128]{1,0:T(8,128)(2,1)} %bitcast.3), custom_call_target="tpu_custom_call" | custom-call | tf_op jit(solution)/shard_map/pallas_call | solution.py:382
  23.9 0.9 %shard_map.38 = f32[4,56,112]{2,1,0:T(8,128)} custom-call(f32[16,8,8,128]{3,2,1,0:T(8,128)S(1)} %get-tuple-element.8.recv, f32[64,512]{1,0:T(8,128)S(1)} %get-tuple-element.9.base, bf16[256,512]{1,0:T(8,128)(2,1)S(1)} %get-tuple-element.10.cvd), custom_call_target="tpu_custom_call" | custom-call | tf_op jit(solution)/shard_map/pallas_call | solution.py:413

commit v8 on v7

--- a/solution.py
+++ b/solution.py
@@ -24,11 +24,12 @@
 GIFT = ROWS_P - OWN
 DEVS = 8
 COLS = 4
-PIECES = ((13, 0, 16), (13, 16, 16), (14, 0, 8), (14, 8, 8), (14, 16, 16), (15, 0, 8), (15, 8, 8), (15, 16, 8), (15, 24, 8))
-SHARED = 14
+PIECES = ((13, 0, 16), (13, 16, 8), (13, 24, 8), (14, 0, 16), (14, 16, 16), (15, 0, 8), (15, 8, 8), (15, 16, 8), (15, 24, 8))
+SIDE = 13
 LAST = STEPS - 1
 LOOPED = STEPS - 3
-GIVEN = 8
+GIFTED = (2, 3, 5, 6, 8, 9, 11, 12)
+GIVEN = len(GIFTED)
 
 
 def iota(shape, dim):
@@ -66,13 +67,13 @@
         pltpu.SemaphoreType.DMA((len(PIECES),)),
         pltpu.SemaphoreType.DMA((2,)),
         pltpu.SemaphoreType.DMA,
-        pltpu.SemaphoreType.DMA((2,)),
-        pltpu.SemaphoreType.DMA((2,)),
-        pltpu.SemaphoreType.DMA((GIVEN + 1,)),
+        pltpu.SemaphoreType.DMA((3,)),
+        pltpu.SemaphoreType.DMA((6,)),
+        pltpu.SemaphoreType.DMA((GIVEN + 4,)),
     )
 
 
-def body(a_hbm, co_hbm, cv_hbm, recv, base, cvd, abuf, land, ends, xbuf, co_ref, cv_ref, lhs1, cv2, w2, w2a, w2b, w2x, cvx, t1, t1x, sendbuf,
+def body(a_hbm, co_hbm, cv_hbm, recv, base, cvd, abuf, land, ends, xbuf, co_ref, cv_ref, lhs1, cv2, w2, w2a, w2b, w2x, w2h, w2g, cvx, t1, t1x, t1h, hbuf, sendx, recvx, sendbuf,
          a_sem, land_sem, l_sem, c_sem, send_sem, recv_sem, give_sem, take_sem):
     row, col = lax.axis_index("dev2"), lax.axis_index("dev")
     me = row * COLS + col
@@ -98,13 +99,15 @@
     cv_copy.start()
     for tile in range(SLOTS):
         fetch(tile).start(priority=1)
-        if tile % 3 == 0:
+        if tile not in GIFTED:
             fetch_rest(tile).start(priority=1)
 
     x, core = col // 2, lax.rem(col, 2)
     far_row, far_x = 1 - row, 1 - x
     giver, taker = (row + x == 2) & (core == 0), (row + x == 2) & (core == 1)
-    plain = row + x < 2
+    last_chip = row + x == 2
+    helper = ((row == 1) & (col == 1)) | ((row == 0) & (col == 3))
+    plain = (row + x < 2) & jnp.logical_not(helper)
     peers = [(far_row, 2 * far_x), (far_row, 2 * far_x + 1), (far_row, 2 * x), (far_row, 2 * x + 1),
              (row, 2 * far_x), (row, 2 * far_x + 1), (row, 2 * x + 1 - core)]
 
@@ -115,12 +118,15 @@
 
     other = 2 * x + 1 - core
     gifts = []
-    for tile in [t for t in range(LOOPED) if t % 3] + [SHARED]:
-        late = tile == SHARED
+    for tile in GIFTED:
         gifts.append(pltpu.make_async_remote_copy(
-            src_ref=a_hbm.at[pl.ds(16, 16) if late else pl.ds(OWN, GIFT), pl.ds(tile * TILE_Q, TILE_Q)],
-            dst_ref=xbuf if late else land.at[tile],
-            send_sem=give_sem.at[1 if late else 0], recv_sem=take_sem.at[len(gifts)],
+            src_ref=a_hbm.at[pl.ds(OWN, GIFT), pl.ds(tile * TILE_Q, TILE_Q)], dst_ref=land.at[tile],
+            send_sem=give_sem.at[0], recv_sem=take_sem.at[len(gifts)],
+            device_id={"dev2": row, "dev": other}, device_id_type=MESH))
+    for k in range(2):
+        gifts.append(pltpu.make_async_remote_copy(
+            src_ref=a_hbm.at[pl.ds(16 + 8 * k, 8), pl.ds(LAST * TILE_Q, TILE_Q)], dst_ref=xbuf.at[pl.ds(8 * k, 8)],
+            send_sem=give_sem.at[1 + k], recv_sem=take_sem.at[GIVEN + k],
             device_id={"dev2": row, "dev": other}, device_id_type=MESH))
     for k in range(GIVEN):
         gifts[k].start()
@@ -128,6 +134,19 @@
     @pl.when(giver)
     def _():
         gifts[GIVEN].start()
+        gifts[GIVEN + 1].start()
+
+    sides = [
+        pltpu.make_async_remote_copy(
+            src_ref=a_hbm.at[pl.ds(first, 4), pl.ds(SIDE * TILE_Q, TILE_Q)], dst_ref=hbuf.at[pl.ds(core * 4, 4)],
+            send_sem=give_sem.at[3 + n], recv_sem=take_sem.at[GIVEN + 2 + core],
+            device_id={"dev2": r, "dev": c}, device_id_type=MESH)
+        for n, (first, r, c) in enumerate([(28, 1, 1), (24, 0, 3)])]
+
+    @pl.when(last_chip)
+    def _():
+        for side in sides:
+            side.start()
 
     co_copy.wait()
     cv_copy.wait()
@@ -140,12 +159,12 @@
 
     co_i = dot(one_hot(iota((32, OCC), 0) % OCC == iota((32, OCC), 1)), co).astype(BF16)
 
-    def spread(dev, groups):
-        width = sum(2 * count * OCC for _, count in groups)
+    def spread(groups):
+        width = sum(2 * count * OCC for _, _, count in groups)
         r, c = iota((NBF, width), 0), iota((NBF, width), 1)
         c32, r32 = iota((32, width), 1), iota((32, width), 0)
         pick, qp, at = r < 0, c32 < 0, 0
-        for first, count in groups:
+        for dev, first, count in groups:
             half = count * OCC
             pick |= (r == dev * ROWS_P + first + (c - at) % half // OCC) & (c >= at) & (c < at + 2 * half)
             qp |= (r32 // OCC % 2 == (c32 - at) // half) & (c32 >= at) & (c32 < at + 2 * half)
@@ -161,9 +180,11 @@
         c32, r32 = iota((32, 256), 1), iota((32, 256), 0)
         keep = (r32 // OCC % 2 == c32 // NBF) & (r32 // 8 == c32 % OCC)
         w2[k] = jnp.where(keep, placed, 0.0).astype(BF16)
-    w2a[...] = spread(col, [(0, 16)])
-    w2b[...] = spread(col, [(16, 8), (24, 8)])
-    w2x[...] = spread(other, [(16, 16)])
+    w2a[...] = spread([(col, 0, 16)])
+    w2b[...] = spread([(col, 16, 8), (col, 24, 8)])
+    w2x[...] = spread([(other, 16, 8), (other, 24, 8)])
+    w2g[...] = spread([(col, 0, 8), (col, 8, 8)])
+    w2h[...] = spread([(2, 24 + 4 * row, 4), (3, 24 + 4 * row, 4)])
 
     b, c = iota((VIRT, 256), 0), iota((VIRT, 256), 1)
     halves = dot_tn(cv, one_hot((b == (c // NBF) * HALF + c % 64) & (c % 64 < HALF)))
@@ -217,6 +238,16 @@
                 device_id={"dev2": r, "dev": c}, device_id_type=MESH).start()
         recv[step, me] = sendbuf[step, me]
 
+    def send_last():
+        for to in range(DEVS):
+            @pl.when(me != to)
+            def _():
+                pltpu.make_async_remote_copy(
+                    src_ref=sendbuf.at[LAST, to], dst_ref=recv.at[LAST, me],
+                    send_sem=send_sem, recv_sem=recv_sem.at[1],
+                    device_id={"dev2": to // COLS, "dev": to % COLS}, device_id_type=MESH).start()
+        recv[LAST, me] = sendbuf[LAST, me]
+
     def blocks(first, count, at):
         return [(qp, first + pb, at + qp * count * OCC + pb * OCC) for qp in range(2) for pb in range(0, count, 4)]
 
@@ -231,7 +262,7 @@
         def _():
             fetch(new).start(priority=1)
 
-        @pl.when((new < LOOPED) & (lax.rem(new, 3) == 0))
+        @pl.when((new < LOOPED) & (lax.rem(new, 3) == 1))
         def _():
             fetch_rest(new).start(priority=1)
 
@@ -239,21 +270,22 @@
             @pl.when(new == step)
             def _():
                 for n in range(len(PIECES)):
-                    if PIECES[n][0] == step and PIECES[n] != (SHARED, 16, 16):
+                    if PIECES[n][0] == step and n not in (2, 7, 8):
                         fetch_piece(n).start(priority=1)
 
-        @pl.when((new == SHARED) & jnp.logical_not(giver))
-        def _():
-            fetch_piece(4).start(priority=1)
-
-    def beside(rows_of, mine, before, weights, more=False):
+        @pl.when((new == SIDE) & jnp.logical_not(last_chip))
+        def _():
+            fetch_piece(2).start(priority=1)
+
+        @pl.when((new == LAST) & jnp.logical_not(giver))
+        def _():
+            fetch_piece(7).start(priority=1)
+            fetch_piece(8).start(priority=1)
+
+    def beside(rows_of, mine, before, weights):
         half = contract_s(t1[...])
-        if more:
-            extra = contract_s(t1x[...])
         contract_r(rows_of, mine[:4])
         e_part = dot(weights, half)
-        if more:
-            e_part += dot(w2x[...], extra)
         contract_r(rows_of, mine[4:])
         pack(before, e_part)
         send(before, 0)
@@ -261,16 +293,16 @@
     def step_body(tile, carry):
         fetch(tile).wait()
 
-        @pl.when(lax.rem(tile, 3) == 0)
+        @pl.when(lax.rem(tile, 3) == 1)
         def _():
             fetch_rest(tile).wait()
 
-        @pl.when(lax.rem(tile, 3) != 0)
+        @pl.when(lax.rem(tile, 3) != 1)
         def _():
             view = land.at[tile]
-            pltpu.make_async_copy(view, view, take_sem.at[tile - tile // 3 - 1]).wait()
-
-        mixed = jnp.where(lax.rem(tile - 1, 3) == 0, 0, 1)
+            pltpu.make_async_copy(view, view, take_sem.at[tile - (tile + 1) // 3 - 1]).wait()
+
+        mixed = jnp.where((lax.rem(tile, 3) == 2) | (tile == 1), 0, 1)
         beside(looped(tile, lax.rem(tile, SLOTS)), whole, tile - 1, w2[mixed])
         refill(tile)
         return carry
@@ -282,65 +314,128 @@
     lax.fori_loop(1, LOOPED, step_body, 0)
 
     fetch_piece(0).wait()
-    beside(ending(LOOPED), upper, LOOPED - 1, w2[0])
-    fetch_piece(1).wait()
-    contract_r(ending(LOOPED), lower)
-    first = [b for b in blocks(0, 16, 0) if b[1] < 8]
-    second = [b for b in blocks(0, 16, 0) if b[1] >= 8]
-
-    @pl.when(giver)
-    def _():
-        fetch_piece(2).wait()
-        beside(ending(SHARED), first, SHARED - 1, w2[0])
-        fetch_piece(3).wait()
-        contract_r(ending(SHARED), second)
-        fetch_piece(5).wait()
-        half = contract_s(t1[:128, :])
-        contract_r(ending(LAST), first)
-        pack(SHARED, dot(w2a[...], half))
-        send(SHARED, 0)
-        fetch_piece(6).wait()
-        contract_r(ending(LAST), second)
-
-    @pl.when(plain)
-    def _():
-        fetch_piece(2).wait()
-        fetch_piece(3).wait()
-        beside(ending(SHARED), upper, SHARED - 1, w2[0])
+    beside(ending(LOOPED), upper, LOOPED - 1, w2[1])
+
+    first = blocks(0, 16, 0)
+
+    def gift_rows(p0, q):
+        return xbuf[p0 - 16:p0 - 14, q]
+
+    def most_of_side():
+        contract_r(ending(SIDE), [b for b in lower if b[1] < 24])
+        for qp in range(2):
+            t1[qp * 128 + 96:(qp + 1) * 128, :] = jnp.zeros((32, 256), BF16)
+
+    def both_halves(before):
+        beside(ending(before + 1), upper, before, w2[0])
         fetch_piece(4).wait()
-        contract_r(ending(SHARED), lower)
+        contract_r(ending(before + 1), lower)
+
+    def start_last():
         fetch_piece(5).wait()
         fetch_piece(6).wait()
-        beside(ending(LAST), first + second, SHARED, w2[0])
+        beside(ending(LAST), first, LAST - 1, w2[0])
+
+    def finish_last(parts, weights, e_part=None):
+        half = jnp.concatenate([contract_s(t1[k:k + 64, :]) for k in parts], axis=0)
+        e_last = dot(weights, half)
+        pack(LAST, e_last if e_part is None else e_part + e_last)
+        send_last()
+
+    @pl.when(giver)
+    def _():
+        fetch_piece(1).wait()
+        most_of_side()
+        fetch_piece(3).wait()
+        both_halves(SIDE)
+        fetch_piece(5).wait()
+        beside(ending(LAST), blocks(0, 8, 0), LAST - 1, w2[0])
+        fetch_piece(6).wait()
+        contract_r(ending(LAST), blocks(8, 8, 64))
+        finish_last((0, 64), w2g[...])
 
     @pl.when(taker)
     def _():
+        fetch_piece(1).wait()
+        gifts[GIVEN].wait_recv()
+        most_of_side()
+        contract_r(gift_rows, blocks(16, 8, 0), t1x)
+        fetch_piece(3).wait()
+        both_halves(SIDE)
+        start_last()
+        fetch_piece(7).wait()
+        gifts[GIVEN + 1].wait_recv()
+        half = contract_s(t1[:128, :])
+        contract_r(ending(LAST), blocks(16, 8, 128))
+        e_part = dot(w2a[...], half)
+        contract_r(gift_rows, blocks(24, 8, 64), t1x)
+        fetch_piece(8).wait()
+        contract_r(ending(LAST), blocks(24, 8, 192))
+        e_part += dot(w2x[...], contract_s(t1x[...]))
+        finish_last((128, 192), w2b[...], e_part)
+
+    @pl.when(plain)
+    def _():
+        fetch_piece(1).wait()
         fetch_piece(2).wait()
+        contract_r(ending(SIDE), lower)
         fetch_piece(3).wait()
-        beside(ending(SHARED), upper, SHARED - 1, w2[0])
-        gifts[GIVEN].wait_recv()
+        both_halves(SIDE)
+
+    @pl.when(helper)
+    def _():
+        fetch_piece(1).wait()
+        fetch_piece(2).wait()
+        for k in range(2):
+            view = hbuf.at[pl.ds(4 * k, 4)]
+            pltpu.make_async_copy(view, view, take_sem.at[GIVEN + 2 + k]).wait()
+        contract_r(ending(SIDE), lower)
+        contract_r(lambda p0, q: hbuf[p0:p0 + 2, q], [(qp, 4 * k, 32 * k + 16 * qp) for k in range(2) for qp in range(2)], t1h)
+        fetch_piece(3).wait()
+        half = contract_s(t1[...])
+        extra = contract_s(t1h[...])
+        contract_r(ending(SIDE + 1), upper[:4])
+        e_part = dot(w2[0], half)
+        e_side = dot(w2h[...], extra)
+        contract_r(ending(SIDE + 1), upper[4:])
+        pack(SIDE, e_part + jnp.where(row == 1, e_side, 0.0))
+        for j in range(OCC):
+            for h in range(2):
+                sendx[2 * j + h] = e_side[8 * j:8 * j + 8, h * NBF:(h + 1) * NBF]
+        send(SIDE, 0)
+
+        @pl.when(row == 0)
+        def _():
+            for r, c in peers:
+                pltpu.make_async_remote_copy(
+                    src_ref=sendx.at[r * COLS + c], dst_ref=recvx, send_sem=give_sem.at[5], recv_sem=recv_sem.at[2],
+                    device_id={"dev2": r, "dev": c}, device_id_type=MESH).start()
+            recvx[...] = sendx[me]
+
         fetch_piece(4).wait()
-        contract_r(ending(SHARED), lower)
-        contract_r(lambda p0, q: xbuf[p0 - 16:p0 - 14, q], blocks(16, 16, 0), t1x)
-        fetch_piece(5).wait()
-        fetch_piece(6).wait()
-        beside(ending(LAST), first + second, SHARED, w2[0], more=True)
-
-    fetch_piece(7).wait()
-    half = contract_s(t1[:128, :])
-    contract_r(ending(LAST), blocks(16, 8, 128))
-    e_part = dot(w2a[...], half)
-    fetch_piece(8).wait()
-    contract_r(ending(LAST), blocks(24, 8, 192))
-    half = jnp.concatenate([contract_s(t1[128:192, :]), contract_s(t1[192:, :])], axis=0)
-    e_part += dot(w2b[...], half)
-    pack(LAST, e_part)
-    send(LAST, 1)
+        contract_r(ending(SIDE + 1), lower)
+
+    @pl.when(jnp.logical_not(last_chip))
+    def _():
+        start_last()
+        fetch_piece(7).wait()
+        half = contract_s(t1[:128, :])
+        contract_r(ending(LAST), blocks(16, 8, 128))
+        e_part = dot(w2a[...], half)
+        fetch_piece(8).wait()
+        contract_r(ending(LAST), blocks(24, 8, 192))
+        finish_last((128, 192), w2b[...], e_part)
 
     def arrived(view, sem):
         pltpu.make_async_copy(view, view, recv_sem.at[sem]).wait()
 
     arrived(recv.at[pl.ds(0, LAST), pl.ds(0, DEVS - 1)], 0)
+
+    @pl.when(me != 3)
+    def _():
+        arrived(recvx, 2)
+
+    recv[SIDE, COLS] = recv[SIDE, COLS] + recvx[...]
     sums = []
     for r in range(2):
         part = recv[:LAST, COLS * r] + recv[:LAST, COLS * r + 1]
@@ -361,6 +456,17 @@
     @pl.when(giver)
     def _():
         gifts[GIVEN].wait_send()
+        gifts[GIVEN + 1].wait_send()
+
+    @pl.when(last_chip)
+    def _():
+        for side in sides:
+            side.wait_send()
+
+    @pl.when(me == 3)
+    def _():
+        view = sendx.at[pl.ds(0, DEVS - 1)]
+        pltpu.make_async_copy(view, view, give_sem.at[5]).wait()
 
 
 def finish(recv, base, cvd, out_ref):
@@ -401,9 +507,15 @@
                 pltpu.VMEM((32, NBF), BF16),
                 pltpu.VMEM((32, NBF), BF16),
                 pltpu.VMEM((32, NBF), BF16),
+                pltpu.VMEM((32, 64), BF16),
+                pltpu.VMEM((32, NBF), BF16),
                 pltpu.VMEM((512, 512), BF16),
                 pltpu.VMEM((256, 256), BF16),
                 pltpu.VMEM((NBF, 256), BF16),
+                pltpu.VMEM((64, 256), BF16),
+                pltpu.VMEM((8, TILE_Q, NBF, NBF), BF16),
+                pltpu.VMEM((DEVS, 8, NBF), F32),
+                pltpu.VMEM((8, NBF), F32),
                 pltpu.VMEM((STEPS, DEVS, 8, NBF), F32),
             ],
             compiler_params=pltpu.CompilerParams(

time: 24.9 us -> 24.8 us (level)
  no operation moved by 1% of the time
where the time goes in v8:
time: 24.8 us; the launch traced here: 24.7 us
  Pallas kernels  24.7 us (100%)
    pallas_call x1, Pallas kernels, local_block(): pl.pallas_call(kernel, out_shape=[jax.ShapeDtypeStruct((STEPS, DEVS, 8, N...  23.8 us
    pallas_call x1, Pallas kernels, local_block(): pl.pallas_call(finish, out_shape=jax.ShapeDtypeStruct((OCC, HALF, VIRT),...  0.88 us

profile of v8, /device:TPU:0, one launch (start us, length us, event | category | flops | bytes accessed | tf_op | source)
XLA Modules:
  0.0 24.7 jit_solution(1458154909426714423)
XLA Ops:
  0.0 23.8 %shard_map.37 = (f32[16,8,8,128]{3,2,1,0:T(8,128)S(1)}, f32[64,512]{1,0:T(8,128)S(1)}, bf16[256,512]{1,0:T(8,128)(2,1)S(1)}) custom-call(bf16[32,64,128,128]{3,2,1,0:T(8,128)(2,1)} %refs_0_.1, bf16[4,128]{1,0:T(4,128)(2,1)} %bitcast.4, bf16[112,128]{1,0:T(8,128)(2,1)} %bitcast.3), custom_call_target="tpu_custom_call" | custom-call | tf_op jit(solution)/shard_map/pallas_call | solution.py:488
  23.8 0.9 %shard_map.38 = f32[4,56,112]{2,1,0:T(8,128)} custom-call(f32[16,8,8,128]{3,2,1,0:T(8,128)S(1)} %get-tuple-element.8.recv, f32[64,512]{1,0:T(8,128)S(1)} %get-tuple-element.9.base, bf16[256,512]{1,0:T(8,128)(2,1)S(1)} %get-tuple-element.10.cvd), custom_call_target="tpu_custom_call" | custom-call | tf_op jit(solution)/shard_map/pallas_call | solution.py:525
